TPU v7x, 8 devices: a whole 2x2x1 slice. The times are simulated.
8 devices in a mesh: dp: 2 (over z, y), tp: 4 (over x, core).
Axes of the slice: x: 2, y: 2, z: 1, core: 2. Of those that a mesh axis runs over, the one named last changes fastest.
Arguments:
- hidden: bfloat16 [8, 5, 2048], P('dp'), parts along dimension 0
- norm_gain: float32 [2048], replicated
- w_head: bfloat16 [2048, 151936], P(None, 'tp')
- draft_probs: float32 [8, 4, 151936], P('dp', None, 'tp'), parts along dimension 0
- draft_tokens: int32 [8, 4], P('dp'), parts along dimension 0
- temperature: float32 [8], P('dp'), parts along dimension 0
Outputs:
- output 1: float32 [8, 4], P('dp'), parts along dimension 0
- output 2: float32 [8, 4], P('dp'), parts along dimension 0
- output 3: float32 [8, 4, 151936], P('dp', None, 'tp'), parts along dimension 0
- output 4: float32 [8], P('dp'), parts along dimension 0
There are 2 independent parts. A program takes and returns all parts, laid end to end along the dimension named above; an argument that names none is the same for every part.
All inputs are finite; a program needn't handle non-finite values.
Results may differ from a plain program's by a relative error of at most 0.001.
Values sent between devices are 32-bit elements.
A program may use at most 1 GiB of HBM per device.

v0:
```python
import jax
import jax.numpy as jnp
from jax import lax
from jax.sharding import PartitionSpec as P


def solution(mesh):
    def local_step(hidden, norm_gain, w_head, draft_probs, draft_tokens, value_a11):
        draft_len = draft_probs.shape[1]
        shard_vocab = w_head.shape[1]
        hidden_f32 = hidden.astype(jnp.float32)
        inv_rms = lax.rsqrt(jnp.mean(hidden_f32 * hidden_f32, axis=-1, keepdims=True) + 1e-5)
        normed = (hidden_f32 * inv_rms * norm_gain).astype(jnp.bfloat16)
        logits = jnp.einsum('cle,ew->clw', normed, w_head, preferred_element_type=jnp.float32)
        scaled = logits / value_a11[:, None, None]
        row_max = lax.pmax(jnp.max(scaled, axis=-1), 'tp')
        local_sum = jnp.sum(jnp.exp(scaled - row_max[:, :, None]), axis=-1)
        local_idx = draft_tokens - lax.axis_index('tp') * shard_vocab
        is_owned = (local_idx >= 0) & (local_idx < shard_vocab)
        safe_idx = jnp.clip(local_idx, 0, shard_vocab - 1)[:, :, None]
        tok_scaled = jnp.where(is_owned, jnp.take_along_axis(scaled[:, :draft_len], safe_idx, axis=-1)[:, :, 0], 0.0)
        tok_draft = jnp.where(is_owned, jnp.take_along_axis(draft_probs, safe_idx, axis=-1)[:, :, 0], 0.0)
        total_sum, tok_scaled, tok_draft = lax.psum((local_sum, tok_scaled, tok_draft), 'tp')
        row_lse = row_max + jnp.log(total_sum)
        draft_lse = row_lse[:, :draft_len]
        tok_target = jnp.exp(tok_scaled - draft_lse)
        accept = jnp.minimum(1.0, tok_target / tok_draft)
        excess = jnp.maximum(jnp.exp(scaled[:, :draft_len] - draft_lse[:, :, None]) - draft_probs, 0.0)
        norm_sum = lax.psum(jnp.sum(excess, axis=-1), 'tp')
        residual = excess / norm_sum[:, :, None]
        return accept, norm_sum, residual, row_lse[:, draft_len]

    return jax.shard_map(
        local_step,
        mesh=mesh,
        in_specs=(P('dp', None, None), P(), P(None, 'tp'), P('dp', None, 'tp'), P('dp', None), P('dp')),
        out_specs=(P('dp', None), P('dp', None), P('dp', None, 'tp'), P('dp')),
        check_vma=False,
    )
```

profile of v0, /device:TPU:0, one launch (start us, length us, event | category | flops | bytes accessed | tf_op | source)
XLA Modules:
  0.0 99.2 jit_solution(13107290463307747540)
XLA Ops:
  0.6 0.7 fusion.16
  1.4 0.1 reshape.58
  1.4 1.5 %gather_fusion.1 = f32[16]{0:T(128)S(1)} fusion(f32[4,4,37984]{2,1,0:T(4,128)} %param.11, s32[16]{0:T(128)S(1)} %reshape.58), kind=kCustom, calls=%fused_computation.1.clone | custom fusion | bytes 320 | tf_op jit(solution)/shard_map/jit(take_along_axis)/gather | solution.py:22
  3.0 0.1 reshape.67
  3.1 1.0 %fusion.5 = f32[4,5]{0,1:T(8,128)S(1)} fusion(bf16[4,5,2048]{2,0,1:T(4,128)(2,1)} %param.8), kind=kLoop, calls=%fused_computation.10 | loop fusion | flops 122860 | bytes 82000 | tf_op jit(solution)/shard_map/reduce_sum | solution.py:12
  4.1 1.0 %fusion.7 = bf16[4,5,2048]{2,0,1:T(4,128)(2,1)S(1)} fusion(bf16[4,5,2048]{2,0,1:T(4,128)(2,1)} %param.8, f32[2048]{0:T(1024)} %param.9, f32[4,5]{0,1:T(8,128)S(1)} %add_rsqrt_fusion), kind=kLoop, calls=%fused_computation.12 | loop fusion | flops 163840 | bytes 172112 | tf_op jit(solution)/shard_map/convert_element_type | solution.py:13
  5.1 57.3 %fusion.17 = (f32[4,5]{1,0:T(4,128)S(1)}, f32[4,5,37984]{2,1,0:T(8,128)}) fusion(f32[4]{0:T(128)} %param.13, bf16[2048,37984]{0,1:T(8,128)(2,1)} %param.10, bf16[4,5,2048]{2,0,1:T(4,128)(2,1)S(1)} %fusion.7), kind=kOutput, calls=%fused_computation.35 | convolution fusion | flops 3113168640 | bytes 158703200 | tf_op jit(solution)/shard_map/cle,ew->clw/dot_general | solution.py:14
  62.4 8.7 %pmax.7 = f32[4,5]{1,0:T(4,128)S(1)} all-reduce(f32[4,5]{1,0:T(4,128)S(1)} %get-tuple-element.13), channel_id=1, replica_groups=mesh['dp'=2,'tp'=4] {'tp'}, use_global_device_ids=true, to_apply=%region_3.5 | all-reduce | flops 20 | bytes 160 | tf_op jit(solution)/shard_map/pmax | solution.py:16
  71.1 0.0 copy-start
  71.1 3.6 %exponential_reduce_fusion = f32[4,5]{1,0:T(4,128)S(1)} fusion(f32[4,5,37984]{2,1,0:T(8,128)} %get-tuple-element.14, f32[4,5]{1,0:T(4,128)S(1)} %pmax.7), kind=kLoop, calls=%fused_computation.5 | loop fusion | flops 1519340 | bytes 3038880 | tf_op jit(solution)/shard_map/reduce_sum | solution.py:17
  74.7 5.7 %psum.29 = f32[4,5]{1,0:T(4,128)S(1)} all-reduce(f32[4,5]{1,0:T(4,128)S(1)} %exponential_reduce_fusion), channel_id=1, replica_groups=mesh['dp'=2,'tp'=4] {'tp'}, use_global_device_ids=true, to_apply=%region_5.7 | all-reduce | flops 20 | bytes 160 | tf_op jit(solution)/shard_map/psum | solution.py:23
  80.4 0.7 slice_reduce_fusion
  81.1 0.0 copy-done
  81.1 0.0 copy-start.1
  81.1 5.1 %fusion.9 = (f32[4,4]{1,0:T(4,128)S(1)}, f32[4,4,37984]{2,1,0:T(4,128)}) fusion(f32[4,4,37984]{2,1,0:T(4,128)S(1)} %copy-done, f32[4,4]{1,0:T(4,128)S(1)} %bitcast.27, f32[4,5,37984]{2,1,0:T(8,128)} %get-tuple-element.14), kind=kLoop, calls=%fused_computation.14 | loop fusion | flops 2430960 | bytes 7293056 | tf_op jit(solution)/shard_map/reduce_sum | solution.py:29
  86.2 1.5 %gather_fusion = f32[16]{0:T(128)S(1)} fusion(f32[4,4,37984]{2,1,0:T(4,128)} %get-tuple-element.12, s32[16]{0:T(128)S(1)} %reshape.58), kind=kCustom, calls=%fused_computation.clone | custom fusion | bytes 320 | tf_op jit(solution)/shard_map/jit(take_along_axis)/gather | solution.py:21
  87.7 0.1 reshape.61
  87.8 0.0 copy-done.1
  87.9 5.8 %all-reduce = (f32[4,4]{1,0:T(4,128)S(1)}, f32[4,4]{1,0:T(4,128)S(1)}, f32[4,4]{1,0:T(4,128)S(1)}) all-reduce(f32[4,4]{1,0:T(4,128)S(1)} %bitcast_select_fusion, f32[4,4]{1,0:T(4,128)S(1)} %get-tuple-element.8, f32[4,4]{1,0:T(4,128)S(1)} %get-tuple-element.11), channel_id=1, replica_groups=mesh['dp'=2,'tp'=4] {'tp'}, use_global_device_ids=true, to_apply=%region_6.8 | all-reduce | flops 48 | bytes 384 | tf_op jit(solution)/shard_map/psum | solution.py:23
  93.7 0.0 copy-start.2
  93.7 4.9 %broadcast_divide_fusion = f32[4,4,37984]{2,1,0:T(4,128)} fusion(f32[4,4]{1,0:T(4,128)S(1)} %get-tuple-element.7, f32[4,4,37984]{2,1,0:T(4,128)S(1)} %copy-done, f32[4,4]{1,0:T(4,128)S(1)} %bitcast.28, f32[4,5,37984]{2,1,0:T(8,128)} %get-tuple-element.14), kind=kLoop, calls=%fused_computation.7 | loop fusion | flops 2430976 | bytes 7293056 | tf_op jit(solution)/shard_map/div | solution.py:30
  98.6 0.0 copy-done.2
  98.6 0.6 fusion.15
  (8 shorter events, 0.1 us)
Async XLA Ops:
  71.1 10.0 %copy-start = (f32[4,4,37984]{2,1,0:T(4,128)S(1)}, f32[4,4,37984]{2,1,0:T(4,128)}, u32[]{:S(2)}) copy-start(f32[4,4,37984]{2,1,0:T(4,128)} %param.11) | copy-start | bytes 7292932
  81.1 6.7 %copy-start.1 = (s32[4,4]{1,0:T(4,128)S(1)}, s32[4,4]{1,0:T(4,128)}, u32[]{:S(2)}) copy-start(s32[4,4]{1,0:T(4,128)} %param.12) | copy-start | bytes 196
  93.7 4.9 %copy-start.2 = (f32[4,4]{1,0:T(4,128)}, f32[4,4]{1,0:T(4,128)S(1)}, u32[]{:S(2)}) copy-start(f32[4,4]{1,0:T(4,128)S(1)} %get-tuple-element.7) | copy-start | bytes 196
where the time goes:
time: 99.8 us; the launch traced here: 99.2 us
  matrix products  57.3 us (57%)
  blocking collectives  20.3 us (20%)
  other arithmetic  16.9 us (17%)
  local copies, waits for them, and re-layouts  4.01 us (4%)
    dot_general x1, matrix products, local_step(): jnp.einsum('cle,ew->clw', normed, w_head, preferred_element_type=jnp.floa...  57.3 us
    psum x2, blocking collectives, local_step(): lax.psum((local_sum, tok_scaled, tok_draft), 'tp')  11.6 us
    pmax x1, blocking collectives, local_step(): row_max = lax.pmax(jnp.max(scaled, axis=-1), 'tp')  8.72 us
    reduce_sum x1, other arithmetic, local_step(): norm_sum = lax.psum(jnp.sum(excess, axis=-1), 'tp')  5.12 us
    div x1, other arithmetic, local_step(): residual = excess / norm_sum[:, :, None]  4.9 us
    reduce_sum x1, other arithmetic, local_step(): local_sum = jnp.sum(jnp.exp(scaled - row_max[:, :, None]), axis=-1)  3.57 us

commit v1 on v0

v1 whole, which is shorter than its diff:
```python
import jax
import jax.numpy as jnp
from jax import lax
from jax.experimental import pallas as pl
from jax.experimental.pallas import tpu as pltpu
from jax.sharding import PartitionSpec as P

MESH = pl.DeviceIdType.MESH
F32 = jnp.float32
LOWEST = float(jnp.finfo(jnp.float32).min)

TILE = 1024
SUB = 256
SLOTS = 4
SHARED = 14
FIRST = 5
PASS = 512


def verify_kernel(
    h_ref, g_ref, t_ref, dt_ref, w_ref, q_ref,
    ex_ref, norm_ref, acc_ref, lse_ref,
    wbuf, wtail, qv, s_scr, xf, xp, xrows, xb, tv, tp_recv, ct, dl, m_scr, l_scr, k_scr,
    zsend, pstat_s, pstat_r, e1s, e1r, e2s, e2r, e3s, e3r,
    w_sem, wt_sem, q_sem, x_sem, t_sem, zs_sem, zr_sem, ps_sem, e1_sem, e2_sem, e3_sem,
):
    dp, tp = lax.axis_index("dp"), lax.axis_index("tp")
    partner = (1 - dp, tp)
    peers = [(dp, lax.rem(tp + d, 4)) for d in (1, 2, 3)]
    n_ids = w_ref.shape[0]
    n_full = n_ids // TILE
    tail = n_ids - n_full * TILE
    tail_at = n_full * TILE
    last = n_full - 2 * SHARED - FIRST
    steps = FIRST + SHARED + last

    def column(i):
        in_shared = (i + steps - FIRST) // steps
        past_shared = (i + steps - FIRST - SHARED) // steps
        return pl.multiple_of((i + in_shared * dp * SHARED + past_shared * (SHARED - dp * SHARED)) * TILE, TILE)

    half = TILE // 2

    def tile_copies(i, slot):
        at = column(i)
        return [
            pltpu.make_async_copy(
                w_ref.at[pl.ds(at + k * half, half), :], wbuf.at[slot, pl.ds(k * half, half), :], w_sem.at[slot, k]
            )
            for k in (0, 1)
        ]

    tail_copy = pltpu.make_async_copy(w_ref.at[pl.ds(tail_at, tail), :], wtail, wt_sem)
    q_copy = pltpu.make_async_copy(q_ref, qv, q_sem)
    for c in tile_copies(0, 0):
        c.start()
    tail_copy.start()
    for i in range(1, SLOTS):
        for c in tile_copies(i, i):
            c.start()
    q_copy.start()

    barrier = pltpu.get_barrier_semaphore()
    for other in [partner] + peers:
        pl.semaphore_signal(barrier, inc=1, device_id=other, device_id_type=MESH)

    h = h_ref[...].astype(F32)
    inv_rms = lax.rsqrt(jnp.mean(h * h, axis=-1, keepdims=True) + 1e-5)
    xf[...] = h * inv_rms * g_ref[...][None]
    for b in range(4):
        tv[0, b : b + 1, :] = jnp.full((1, 128), 1.0, F32) / jnp.full((1, 128), t_ref[b], F32)
        for j in range(4):
            tv[1 + j, b : b + 1, :] = jnp.full((1, 128), dt_ref[b, j].astype(F32), F32)

    def lay_rows(src, t_src, at):
        xrows[...] = jnp.zeros_like(xrows)
        lane = lax.broadcasted_iota(jnp.int32, (1, 128), 1) + tp * n_ids
        for b in range(4):
            for j in range(5):
                xrows[8 * b + j : 8 * b + j + 1, :] = src[j, b : b + 1, :]
            ct[at + 8 * b : at + 8 * b + 8, :] = jnp.broadcast_to(t_src[0, b : b + 1, :], (8, 128))
            dl[at + 8 * b : at + 8 * b + 8, :] = jnp.full((8, 128), -1.0, F32)
            for j in range(4):
                dl[at + 8 * b + j : at + 8 * b + j + 1, :] = t_src[1 + j, b : b + 1, :] - lane.astype(F32)
        xb[at : at + 32, :] = xrows[...].astype(jnp.bfloat16)

    lay_rows(xf, tv, 0)
    m_scr[...] = jnp.full(m_scr.shape, LOWEST, F32)
    l_scr[...] = jnp.zeros_like(l_scr)
    k_scr[...] = jnp.zeros_like(k_scr)

    pl.semaphore_wait(barrier, 4)
    x_copy = pltpu.make_async_remote_copy(
        src_ref=xf, dst_ref=xp, send_sem=x_sem.at[0], recv_sem=x_sem.at[1], device_id=partner, device_id_type=MESH
    )
    t_copy = pltpu.make_async_remote_copy(
        src_ref=tv, dst_ref=tp_recv, send_sem=t_sem.at[0], recv_sem=t_sem.at[1], device_id=partner, device_id_type=MESH
    )
    x_copy.start()
    t_copy.start()

    def product(rows, w):
        return lax.dot_general(xb[0:rows, :], w, (((1,), (1,)), ((), ())), preferred_element_type=F32)

    def fold(rows, parts):
        m_old = m_scr[0:rows, :]
        m_new = m_old
        for p in parts:
            m_new = jnp.maximum(m_new, p)
        total = l_scr[0:rows, :] * jnp.exp(m_old - m_new)
        for p in parts:
            total = total + jnp.exp(p - m_new)
        m_scr[0:rows, :] = m_new
        l_scr[0:rows, :] = total

    tail_copy.wait()
    z = product(32, wtail[...])
    s = z * ct[0:32, 0:tail]
    for b in range(4):
        s_scr[b, :, tail_at : tail_at + tail] = s[8 * b : 8 * b + 4, :]
    k_scr[0:32, 0:tail] = jnp.where(dl[0:32, 0:tail] == float(tail_at), s, 0.0)
    m_tail = jnp.max(s, axis=1, keepdims=True)
    l_tail = jnp.sum(jnp.exp(s - m_tail), axis=1, keepdims=True)
    lane0 = lax.broadcasted_iota(jnp.int32, (32, 128), 1) == 0
    m_scr[0:32, :] = jnp.where(lane0, m_tail, LOWEST)
    l_scr[0:32, :] = jnp.where(lane0, l_tail, 0.0)

    def z_copy(k):
        at = column(FIRST + k)
        return pltpu.make_async_remote_copy(
            src_ref=zsend.at[k], dst_ref=s_scr.at[:, :, pl.ds(at, TILE)], send_sem=zs_sem.at[k], recv_sem=zr_sem.at[k],
            device_id=partner, device_id_type=MESH,
        )

    def step(i, rows):
        slot = i % SLOTS
        for c in tile_copies(i, slot):
            c.wait()
        if rows == 64:
            k = i - FIRST

            @pl.when(k > 0)
            def _():
                z_copy(k - 1).start()

        at = column(i)
        kept = k_scr[0:rows, :]
        for c in range(TILE // SUB):
            z = product(rows, wbuf[slot, c * SUB : (c + 1) * SUB, :])
            parts = []
            for lane in range(0, SUB, 128):
                s = z[:, lane : lane + 128] * ct[0:rows, :]
                parts.append(s)
                off = c * SUB + lane
                kept = jnp.where(dl[0:rows, :] == (at + off).astype(F32), s, kept)
                for b in range(4):
                    s_scr[b, :, pl.ds(at + off, 128)] = s[8 * b : 8 * b + 4, :]
                    if rows == 64:
                        zsend[k, b, :, off : off + 128] = s[32 + 8 * b : 32 + 8 * b + 4, :]
            fold(rows, parts)
        k_scr[0:rows, :] = kept

        @pl.when(i + SLOTS < steps)
        def _():
            for c in tile_copies(i + SLOTS, slot):
                c.start()

    lax.fori_loop(0, FIRST, lambda i, _: step(i, 32), None)
    x_copy.wait()
    t_copy.wait()
    lay_rows(xp, tp_recv, 32)
    lax.fori_loop(FIRST, FIRST + SHARED, lambda i, _: step(i, 64), None)
    pstat_s[0] = m_scr[32:64, :]
    pstat_s[1] = l_scr[32:64, :]
    pstat_s[2] = k_scr[32:64, :]
    z_copy(SHARED - 1).start()
    stat_copy = pltpu.make_async_remote_copy(
        src_ref=pstat_s, dst_ref=pstat_r, send_sem=ps_sem.at[0], recv_sem=ps_sem.at[1],
        device_id=partner, device_id_type=MESH,
    )
    stat_copy.start()
    lax.fori_loop(FIRST + SHARED, steps, lambda i, _: step(i, 32), None)

    group = lax.broadcasted_iota(jnp.int32, (8, 128), 1) // 32

    def pack(cols):
        size = cols[0].shape[0]
        packed = jnp.broadcast_to(cols[0], (size, 128))
        for b in range(1, 4):
            packed = jnp.where(group[:size] == b, cols[b], packed)
        return packed

    def unpack(packed, b):
        size = packed.shape[0]
        lane = lax.broadcasted_iota(jnp.int32, (size, 128), 1)
        return jnp.sum(jnp.where(lane == 32 * b, packed, 0.0), axis=1, keepdims=True)

    def exchange(src, dst, sem):
        return [
            pltpu.make_async_remote_copy(
                src_ref=src, dst_ref=dst.at[d], send_sem=sem.at[0, d], recv_sem=sem.at[1, d],
                device_id=peers[d], device_id_type=MESH,
            )
            for d in range(3)
        ]

    stat_copy.wait()
    m = jnp.maximum(m_scr[0:32, :], pstat_r[0])
    total = l_scr[0:32, :] * jnp.exp(m_scr[0:32, :] - m) + pstat_r[1] * jnp.exp(pstat_r[0] - m)
    row_max = jnp.max(m, axis=1, keepdims=True)
    row_lse = row_max + jnp.log(jnp.sum(total * jnp.exp(m - row_max), axis=1, keepdims=True))
    e1s[...] = pack([row_lse[8 * b : 8 * b + 8, :] for b in range(4)])
    e1 = exchange(e1s, e1r, e1_sem)
    for c in e1:
        c.start()

    q_copy.wait()
    own = [dl[8 * b : 8 * b + 4, :] for b in range(4)]

    def pick(i, found):
        at = pl.multiple_of(i * PASS, PASS)
        out = []
        for b in range(4):
            f = found[b]
            for off in range(0, PASS, 128):
                f = jnp.where(own[b] == (at + off).astype(F32), qv[b, :, pl.ds(at + off, 128)], f)
            out.append(f)
        return tuple(out)

    zero = jnp.zeros((4, 128), F32)
    found = lax.fori_loop(0, tail_at // PASS, pick, (zero,) * 4)
    token_q, token_s = [], []
    for b in range(4):
        f = jnp.where(own[b][:, :tail] == float(tail_at), qv[b, :, tail_at : tail_at + tail], 0.0)
        token_q.append(jnp.sum(found[b], axis=1, keepdims=True) + jnp.sum(f, axis=1, keepdims=True))
        kept = k_scr[8 * b : 8 * b + 4, :] + pstat_r[2, 8 * b : 8 * b + 4, :]
        token_s.append(jnp.sum(kept, axis=1, keepdims=True))
    e3s[0] = pack(token_s)
    e3s[1] = pack(token_q)
    e3 = exchange(e3s, e3r, e3_sem)
    for c in e3:
        c.start()

    def await_z(k, _):
        z_copy(k).wait_send()
        pltpu.make_async_remote_copy(
            src_ref=zsend.at[k], dst_ref=s_scr.at[:, :, pl.ds(pl.multiple_of((FIRST + (1 - dp) * SHARED + k) * TILE, TILE), TILE)],
            send_sem=zs_sem.at[k], recv_sem=zr_sem.at[k], device_id=partner, device_id_type=MESH,
        ).wait_recv()
        return None

    lax.fori_loop(0, SHARED, await_z, None)
    for c in e1:
        c.wait()
    lses = [e1s[...]] + [e1r[d] for d in range(3)]
    top = jnp.maximum(jnp.maximum(lses[0], lses[1]), jnp.maximum(lses[2], lses[3]))
    sums = jnp.exp(lses[0] - top) + jnp.exp(lses[1] - top) + jnp.exp(lses[2] - top) + jnp.exp(lses[3] - top)
    lse = top + jnp.log(sums)
    lse_ref[...] = lse
    row_l = [jnp.broadcast_to(unpack(lse[0:4, :], b), (4, 128)) for b in range(4)]

    def excess(b, at, size):
        e = jnp.maximum(jnp.exp(s_scr[b, :, pl.ds(at, size)] - row_l[b][:, :size]) - qv[b, :, pl.ds(at, size)], 0.0)
        ex_ref[b, :, pl.ds(at, size)] = e
        return e

    def last_pass(i, sums):
        at = pl.multiple_of(i * PASS, PASS)
        out = []
        for b in range(4):
            acc = sums[b]
            for off in range(0, PASS, 128):
                acc = acc + excess(b, at + off, 128)
            out.append(acc)
        return tuple(out)

    sums = lax.fori_loop(0, tail_at // PASS, last_pass, (zero,) * 4)
    rows = []
    for b in range(4):
        e = excess(b, tail_at, tail)
        rows.append(jnp.sum(sums[b], axis=1, keepdims=True) + jnp.sum(e, axis=1, keepdims=True))
    e2s[...] = pack(rows)
    e2 = exchange(e2s, e2r, e2_sem)
    for c in e2:
        c.start()

    for c in e3:
        c.wait()
    at_token = (e3s[...] + e3r[0]) + (e3r[1] + e3r[2])
    acc_ref[...] = jnp.minimum(jnp.exp(at_token[0] - lse[0:4, :]) / at_token[1], 1.0)

    for c in e2:
        c.wait()
    norm = (e2s[...] + e2r[0]) + (e2r[1] + e2r[2])
    for b in range(4):
        norm_ref[b] = jnp.broadcast_to(unpack(norm, b), (4, 128))


def solution(mesh):
    def local_step(hidden, norm_gain, w_head, draft_probs, draft_tokens, temperature):
        n_ids = w_head.shape[1]
        width = w_head.shape[0]
        pad_ids = -(-n_ids // 128) * 128
        tail = n_ids % TILE
        vmem, smem, hbm = pltpu.VMEM, pltpu.SMEM, pltpu.HBM
        dma = pltpu.SemaphoreType.DMA
        ex, norm, acc, lse = pl.pallas_call(
            verify_kernel,
            out_shape=[
                jax.ShapeDtypeStruct((4, 4, n_ids), F32),
                jax.ShapeDtypeStruct((4, 4, 128), F32),
                jax.ShapeDtypeStruct((4, 128), F32),
                jax.ShapeDtypeStruct((8, 128), F32),
            ],
            in_specs=[pl.BlockSpec(memory_space=s) for s in (vmem, vmem, smem, smem, hbm, hbm)],
            out_specs=[pl.BlockSpec(memory_space=vmem)] * 4,
            scratch_shapes=[
                vmem((SLOTS, TILE, width), jnp.bfloat16),
                vmem((tail, width), jnp.bfloat16),
                vmem((4, 4, n_ids), F32),
                vmem((4, 4, pad_ids), F32),
                vmem((5, 4, width), F32),
                vmem((5, 4, width), F32),
                vmem((32, width), F32),
                vmem((64, width), jnp.bfloat16),
                vmem((5, 4, 128), F32),
                vmem((5, 4, 128), F32),
                vmem((64, 128), F32),
                vmem((64, 128), F32),
                vmem((64, 128), F32),
                vmem((64, 128), F32),
                vmem((64, 128), F32),
                vmem((SHARED, 4, 4, TILE), F32),
                vmem((3, 32, 128), F32),
                vmem((3, 32, 128), F32),
                vmem((8, 128), F32),
                vmem((3, 8, 128), F32),
                vmem((4, 128), F32),
                vmem((3, 4, 128), F32),
                vmem((2, 4, 128), F32),
                vmem((3, 2, 4, 128), F32),
                dma((SLOTS, 2)), dma, dma, dma((2,)), dma((2,)), dma((SHARED,)), dma((SHARED,)), dma((2,)),
                dma((2, 3)), dma((2, 3)), dma((2, 3)),
            ],
            compiler_params=pltpu.CompilerParams(collective_id=0, has_side_effects=True),
            name="verify",
        )(
            hidden.transpose(1, 0, 2), norm_gain.reshape(1, width), temperature, draft_tokens,
            w_head.T, draft_probs,
        )
        residual = ex / norm[:, :, :1]
        return acc[:, ::32].T, norm[:, :, 0], residual, lse[4, ::32]

    return jax.shard_map(
        local_step,
        mesh=mesh,
        in_specs=(P("dp", None, None), P(), P(None, "tp"), P("dp", None, "tp"), P("dp", None), P("dp")),
        out_specs=(P("dp", None), P("dp", None), P("dp", None, "tp"), P("dp")),
        check_vma=False,
    )
```

time: 99.8 us -> 58.2 us (0.58)
  matrix products: 57.3 us -> 0 us
  Pallas kernels: 0 us -> 50.2 us
  blocking collectives: 20.3 us -> 0 us
  other arithmetic: 16.9 us -> 3.6 us
    dot_general x1 -> x0, matrix products: 57.3 us -> none  [local_step(): jnp.einsum('cle,ew->clw', normed, w_head, preferred_element_type=jnp.floa...]
    pallas_call x0 -> x1, Pallas kernels: none -> 50.2 us  [local_step(): pl.pallas_call(verify_kernel, out_shape=[jax.ShapeDtypeStruct((4, 4, n_id...]
    psum x2 -> x0, blocking collectives: 11.6 us -> none  [local_step(): lax.psum((local_sum, tok_scaled, tok_draft), 'tp')]
    reduce_sum x3 -> x0, other arithmetic: 9.72 us -> none  [the longest x1 5.12 us: local_step(): norm_sum = lax.psum(jnp.sum(excess, axis=-1), 'tp')]
    pmax x1 -> x0, blocking collectives: 8.72 us -> none  [local_step(): row_max = lax.pmax(jnp.max(scaled, axis=-1), 'tp')]
    gather x5 -> x0, local copies, waits for them, and re-layouts: 3.29 us -> none  [the longest x3 1.68 us: local_step(): jnp.take_along_axis(scaled[:, :draft_len], safe_idx, axis=-1)[:, :, 0]]
    slice x1 -> x3, local copies, waits for them, and re-layouts: 0.7 us -> 2.79 us  [local_step(): return (acc[:, ::32].T, norm[:, :, 0], residual, lse[4, ::32])]
    div x1, other arithmetic: 4.9 us -> 3.6 us  [local_step(): residual = ex / norm[:, :, :1]]
where the time goes in v1:
time: 58.2 us; the launch traced here: 57.9 us
  Pallas kernels  50.2 us (86%)
  other arithmetic  3.6 us (6%)
  local copies, waits for them, and re-layouts  3.46 us (6%)
  between operations  0.64 us (1%)
    pallas_call x1, Pallas kernels, local_step(): pl.pallas_call(verify_kernel, out_shape=[jax.ShapeDtypeStruct((4, 4, n_id...  50.2 us
    div x1, other arithmetic, local_step(): residual = ex / norm[:, :, :1]  3.6 us
    slice x3, local copies, waits for them, and re-layouts, local_step(): return (acc[:, ::32].T, norm[:, :, 0], residual, lse[4, ::32])  2.79 us

profile of v1, /device:TPU:0, one launch (start us, length us, event | category | flops | bytes accessed | tf_op | source)
XLA Modules:
  0.0 57.9 jit_solution(17128512115327017027)
XLA Ops:
  0.6 50.2 %verify.1 = (f32[4,4,37984]{2,1,0:T(4,128)}, f32[4,4,128]{2,1,0:T(4,128)}, f32[4,128]{1,0:T(4,128)}, f32[8,128]{1,0:T(8,128)}) custom-call(bf16[5,4,2048]{2,1,0:T(4,128)(2,1)} %bitcast.5, f32[1,2048]{1,0:T(1,128)} %bitcast.6, f32[4]{0:T(128)} %t_ref.1, s32[4,4]{1,0:T(4,128)} %dt_ref.1, bf16[37984,2048]{1,0:T(8,128)(2,1)} %bitcast.2.w_ref, f32[4,4,37984]{2,1,0:T(4,128)} %q_ref.1), custom_call_target="tpu_custom_call" | custom-call | tf_op jit(solution)/shard_map/verify/pallas_call | solution.py:307
  50.8 0.7 %slice.10 = f32[4,4]{1,0:T(4,128)S(1)} slice(f32[4,128]{1,0:T(4,128)} %get-tuple-element.8), slice={[0:4:1], [0:128:32]} | slice | bytes 128 | tf_op jit(solution)/shard_map/slice | solution.py:352
  51.6 0.7 %copy.11 = f32[4,4]{1,0:T(4,128)} copy(f32[4,4]{0,1:T(4,128)S(1)} %bitcast.7) | data formatting | bytes 128
  52.3 1.3 %slice.12 = f32[1,4]{1,0:T(1,128)} slice(f32[8,128]{1,0:T(8,128)} %get-tuple-element.11), slice={[4:5:1], [0:128:32]} | slice | bytes 32 | tf_op jit(solution)/shard_map/slice | solution.py:352
  53.5 0.8 %slice_reduce_fusion = f32[4,4]{1,0:T(4,128)S(1)} fusion(f32[4,4,128]{2,1,0:T(4,128)} %get-tuple-element.9), kind=kLoop, calls=%fused_computation.1 | loop fusion | bytes 128 | tf_op jit(solution)/shard_map/slice | solution.py:352
  54.3 0.0 copy-start
  54.3 3.6 %broadcast_divide_fusion = f32[4,4,37984]{2,1,0:T(4,128)} fusion(f32[4,4,37984]{2,1,0:T(4,128)} %get-tuple-element.10, f32[4,4]{1,0:T(4,128)S(1)} %slice_reduce_fusion), kind=kLoop, calls=%fused_computation | loop fusion | flops 607744 | bytes 4862016 | tf_op jit(solution)/shard_map/div | solution.py:351
  57.9 0.0 copy-done
Async XLA Ops:
  54.3 3.6 %copy-start = (f32[4,4]{1,0:T(4,128)}, f32[4,4]{1,0:T(4,128)S(1)}, u32[]{:S(2)}) copy-start(f32[4,4]{1,0:T(4,128)S(1)} %slice_reduce_fusion) | copy-start | bytes 196

commit v2 on v1

--- a/solution.py
+++ b/solution.py
@@ -12,7 +12,7 @@
 TILE = 1024
 SUB = 256
 SLOTS = 4
-SHARED = 14
+SHARED = 8
 FIRST = 5
 PASS = 512
 
@@ -291,9 +291,50 @@
 
     for c in e2:
         c.wait()
-    norm = (e2s[...] + e2r[0]) + (e2r[1] + e2r[2])
+    norm_ref[...] = (e2s[...] + e2r[0]) + (e2r[1] + e2r[2])
+
+
+def finish_kernel(
+    ex_ref, norm_ref, acc_ref, lse_ref, acc_out, norm_out, res_out, bonus_out, acc_v, norm_v, bonus_v, stage, sem, r_sem
+):
+    n_ids = ex_ref.shape[2]
+    n_full = n_ids // PASS
+    lane = lax.broadcasted_iota(jnp.int32, (4, 128), 1)
+    norm = norm_ref[...]
+    writes = []
     for b in range(4):
-        norm_ref[b] = jnp.broadcast_to(unpack(norm, b), (4, 128))
+        total = jnp.sum(jnp.where(lane == 32 * b, norm, 0.0), axis=1, keepdims=True)
+        scale = jnp.broadcast_to(1.0 / jnp.broadcast_to(total, (4, 128)), (4, 128))
+
+        def body(i, _):
+            at = pl.multiple_of(i * PASS, PASS)
+            for off in range(0, PASS, 128):
+                stage[b, :, pl.ds(at + off, 128)] = ex_ref[b, :, pl.ds(at + off, 128)] * scale
+
+        lax.fori_loop(0, n_full, body, None)
+        for at in range(n_full * PASS, n_ids, 128):
+            size = min(128, n_ids - at)
+            stage[b, :, at : at + size] = ex_ref[b, :, at : at + size] * scale[:, :size]
+        writes.append(pltpu.make_async_copy(stage.at[b], res_out.at[b], r_sem.at[b]))
+        writes[-1].start()
+
+    sub = lax.broadcasted_iota(jnp.int32, (4, 128), 0)
+    for src, dst, out, k in ((acc_ref[...], acc_v, acc_out, 0), (norm, norm_v, norm_out, 1)):
+        row = jnp.sum(jnp.where(lane % 32 == sub, src, 0.0), axis=0, keepdims=True)
+        for b in range(4):
+            dst[b : b + 1, :] = (row if b == 0 else pltpu.roll(row, 128 - 32 * b, 1))[:, 0:4]
+        writes.append(pltpu.make_async_copy(dst, out, sem.at[k]))
+        writes[-1].start()
+    row = lse_ref[4:5, :]
+    lane = lane[0:1, :]
+    packed = row
+    for b in range(1, 4):
+        packed = jnp.where(lane == b, pltpu.roll(row, 128 - 31 * b, 1), packed)
+    bonus_v[...] = packed[:, 0:4]
+    writes.append(pltpu.make_async_copy(bonus_v, bonus_out, sem.at[2]))
+    writes[-1].start()
+    for c in writes:
+        c.wait()
 
 
 def solution(mesh):
@@ -306,12 +347,7 @@
         dma = pltpu.SemaphoreType.DMA
         ex, norm, acc, lse = pl.pallas_call(
             verify_kernel,
-            out_shape=[
-                jax.ShapeDtypeStruct((4, 4, n_ids), F32),
-                jax.ShapeDtypeStruct((4, 4, 128), F32),
-                jax.ShapeDtypeStruct((4, 128), F32),
-                jax.ShapeDtypeStruct((8, 128), F32),
-            ],
+            out_shape=[vmem((4, 4, n_ids), F32), vmem((4, 128), F32), vmem((4, 128), F32), vmem((8, 128), F32)],
             in_specs=[pl.BlockSpec(memory_space=s) for s in (vmem, vmem, smem, smem, hbm, hbm)],
             out_specs=[pl.BlockSpec(memory_space=vmem)] * 4,
             scratch_shapes=[
@@ -348,8 +384,23 @@
             hidden.transpose(1, 0, 2), norm_gain.reshape(1, width), temperature, draft_tokens,
             w_head.T, draft_probs,
         )
-        residual = ex / norm[:, :, :1]
-        return acc[:, ::32].T, norm[:, :, 0], residual, lse[4, ::32]
+        acc, norm, residual, bonus = pl.pallas_call(
+            finish_kernel,
+            out_shape=[
+                jax.ShapeDtypeStruct((4, 4), F32),
+                jax.ShapeDtypeStruct((4, 4), F32),
+                jax.ShapeDtypeStruct((4, 4, n_ids), F32),
+                jax.ShapeDtypeStruct((1, 4), F32),
+            ],
+            in_specs=[pl.BlockSpec(memory_space=vmem)] * 4,
+            out_specs=[pl.BlockSpec(memory_space=hbm)] * 4,
+            scratch_shapes=[
+                vmem((4, 4), F32), vmem((4, 4), F32), vmem((1, 4), F32), vmem((4, 4, n_ids), F32), dma((3,)), dma((4,)),
+            ],
+            compiler_params=pltpu.CompilerParams(vmem_limit_bytes=16 * 1024 * 1024),
+            name="finish",
+        )(ex, norm, acc, lse)
+        return acc, norm, residual, bonus.reshape(4)
 
     return jax.shard_map(
         local_step,

time: 58.2 us -> 61.5 us (1.057)
  Pallas kernels: 50.2 us -> 60.7 us
  other arithmetic: 3.6 us -> 0 us
  local copies, waits for them, and re-layouts: 3.46 us -> 0 us
    pallas_call x1 -> x2, Pallas kernels: 50.2 us -> 60.7 us  [the longest x1 56.5 us: local_step(): pl.pallas_call(verify_kernel, out_shape=[vmem((4, 4, n_ids), F32), vmem((...]
    div x1 -> x0, other arithmetic: 3.6 us -> none  [local_step(): residual = ex / norm[:, :, :1]]
    slice x3 -> x0, local copies, waits for them, and re-layouts: 2.79 us -> none  [local_step(): return (acc[:, ::32].T, norm[:, :, 0], residual, lse[4, ::32])]
    unnamed x3 -> x0, local copies, waits for them, and re-layouts: 0.67 us -> none
where the time goes in v2:
time: 61.5 us; the launch traced here: 61.4 us
  Pallas kernels  60.7 us (99%)
  between operations  0.64 us (1%)
    pallas_call x1, Pallas kernels, local_step(): pl.pallas_call(verify_kernel, out_shape=[vmem((4, 4, n_ids), F32), vmem((...  56.5 us
    pallas_call x1, Pallas kernels, local_step(): pl.pallas_call(finish_kernel, out_shape=[jax.ShapeDtypeStruct((4, 4), F32...  4.23 us

profile of v2, /device:TPU:0, one launch (start us, length us, event | category | flops | bytes accessed | tf_op | source)
XLA Modules:
  0.0 61.4 jit_solution(17127777632196714369)
XLA Ops:
  0.6 56.5 %verify.1 = (f32[4,4,37984]{2,1,0:T(4,128)S(1)}, f32[4,128]{1,0:T(4,128)S(1)}, f32[4,128]{1,0:T(4,128)S(1)}, f32[8,128]{1,0:T(8,128)S(1)}) custom-call(bf16[5,4,2048]{2,1,0:T(4,128)(2,1)} %bitcast.4, f32[1,2048]{1,0:T(1,128)} %bitcast.5, f32[4]{0:T(128)} %t_ref.1, s32[4,4]{1,0:T(4,128)} %dt_ref.1, bf16[37984,2048]{1,0:T(8,128)(2,1)} %bitcast.2.w_ref, ...), custom_call_target="tpu_custom_call" | custom-call | tf_op jit(solution)/shard_map/verify/pallas_call | solution.py:348
  57.2 4.2 %finish.1 = (f32[4,4]{1,0:T(4,128)}, f32[4,4]{1,0:T(4,128)}, f32[4,4,37984]{2,1,0:T(4,128)}, f32[1,4]{1,0:T(1,128)}) custom-call(f32[4,4,37984]{2,1,0:T(4,128)S(1)} %get-tuple-element.12.ex_ref, f32[4,128]{1,0:T(4,128)S(1)} %get-tuple-element.13.norm_ref, f32[4,128]{1,0:T(4,128)S(1)} %get-tuple-element.14.acc_ref, f32[8,128]{1,0:T(8,128)S(1)} %get-tuple-element.15.lse_ref), custom_call_target="tpu_custom_call" | custom-call | tf_op jit(solution)/shard_map/finish/pallas_call | solution.py:387

commit v3 on v2

--- a/solution.py
+++ b/solution.py
@@ -12,17 +12,17 @@
 TILE = 1024
 SUB = 256
 SLOTS = 4
-SHARED = 8
+SHARED = 14
 FIRST = 5
-PASS = 512
+PASS = 1024
 
 
 def verify_kernel(
-    h_ref, g_ref, t_ref, dt_ref, w_ref, q_ref,
+    h_hbm, g_hbm, t_hbm, dt_hbm, w_ref, q_ref,
     ex_ref, norm_ref, acc_ref, lse_ref,
-    wbuf, wtail, qv, s_scr, xf, xp, xrows, xb, tv, tp_recv, ct, dl, m_scr, l_scr, k_scr,
+    h_ref, g_ref, t_ref, dt_ref, wbuf, wtail, qv, s_scr, xf, xp, xrows, xb, tv, tp_recv, ct, dl, m_scr, l_scr, k_scr,
     zsend, pstat_s, pstat_r, e1s, e1r, e2s, e2r, e3s, e3r,
-    w_sem, wt_sem, q_sem, x_sem, t_sem, zs_sem, zr_sem, ps_sem, e1_sem, e2_sem, e3_sem,
+    in_sem, w_sem, wt_sem, q_sem, x_sem, t_sem, zs_sem, zr_sem, ps_sem, e1_sem, e2_sem, e3_sem,
 ):
     dp, tp = lax.axis_index("dp"), lax.axis_index("tp")
     partner = (1 - dp, tp)
@@ -52,10 +52,14 @@
 
     tail_copy = pltpu.make_async_copy(w_ref.at[pl.ds(tail_at, tail), :], wtail, wt_sem)
     q_copy = pltpu.make_async_copy(q_ref, qv, q_sem)
-    for c in tile_copies(0, 0):
+    small = [
+        pltpu.make_async_copy(src, dst, in_sem.at[k])
+        for k, (src, dst) in enumerate(((h_hbm, h_ref), (g_hbm, g_ref), (t_hbm, t_ref), (dt_hbm, dt_ref)))
+    ]
+    for c in small:
         c.start()
     tail_copy.start()
-    for i in range(1, SLOTS):
+    for i in range(SLOTS):
         for c in tile_copies(i, i):
             c.start()
     q_copy.start()
@@ -64,6 +68,8 @@
     for other in [partner] + peers:
         pl.semaphore_signal(barrier, inc=1, device_id=other, device_id_type=MESH)
 
+    for c in small:
+        c.wait()
     h = h_ref[...].astype(F32)
     inv_rms = lax.rsqrt(jnp.mean(h * h, axis=-1, keepdims=True) + 1e-5)
     xf[...] = h * inv_rms * g_ref[...][None]
@@ -298,7 +304,6 @@
     ex_ref, norm_ref, acc_ref, lse_ref, acc_out, norm_out, res_out, bonus_out, acc_v, norm_v, bonus_v, stage, sem, r_sem
 ):
     n_ids = ex_ref.shape[2]
-    n_full = n_ids // PASS
     lane = lax.broadcasted_iota(jnp.int32, (4, 128), 1)
     norm = norm_ref[...]
     writes = []
@@ -306,13 +311,7 @@
         total = jnp.sum(jnp.where(lane == 32 * b, norm, 0.0), axis=1, keepdims=True)
         scale = jnp.broadcast_to(1.0 / jnp.broadcast_to(total, (4, 128)), (4, 128))
 
-        def body(i, _):
-            at = pl.multiple_of(i * PASS, PASS)
-            for off in range(0, PASS, 128):
-                stage[b, :, pl.ds(at + off, 128)] = ex_ref[b, :, pl.ds(at + off, 128)] * scale
-
-        lax.fori_loop(0, n_full, body, None)
-        for at in range(n_full * PASS, n_ids, 128):
+        for at in range(0, n_ids, 128):
             size = min(128, n_ids - at)
             stage[b, :, at : at + size] = ex_ref[b, :, at : at + size] * scale[:, :size]
         writes.append(pltpu.make_async_copy(stage.at[b], res_out.at[b], r_sem.at[b]))
@@ -348,9 +347,13 @@
         ex, norm, acc, lse = pl.pallas_call(
             verify_kernel,
             out_shape=[vmem((4, 4, n_ids), F32), vmem((4, 128), F32), vmem((4, 128), F32), vmem((8, 128), F32)],
-            in_specs=[pl.BlockSpec(memory_space=s) for s in (vmem, vmem, smem, smem, hbm, hbm)],
+            in_specs=[pl.BlockSpec(memory_space=s) for s in (hbm,) * 6],
             out_specs=[pl.BlockSpec(memory_space=vmem)] * 4,
             scratch_shapes=[
+                vmem((5, 4, width), jnp.bfloat16),
+                vmem((1, width), F32),
+                smem((4,), F32),
+                smem((4, 4), jnp.int32),
                 vmem((SLOTS, TILE, width), jnp.bfloat16),
                 vmem((tail, width), jnp.bfloat16),
                 vmem((4, 4, n_ids), F32),
@@ -375,7 +378,7 @@
                 vmem((3, 4, 128), F32),
                 vmem((2, 4, 128), F32),
                 vmem((3, 2, 4, 128), F32),
-                dma((SLOTS, 2)), dma, dma, dma((2,)), dma((2,)), dma((SHARED,)), dma((SHARED,)), dma((2,)),
+                dma((4,)), dma((SLOTS, 2)), dma, dma, dma((2,)), dma((2,)), dma((SHARED,)), dma((SHARED,)), dma((2,)),
                 dma((2, 3)), dma((2, 3)), dma((2, 3)),
             ],
             compiler_params=pltpu.CompilerParams(collective_id=0, has_side_effects=True),

time: 61.5 us -> 50.1 us (0.81)
  Pallas kernels: 60.7 us -> 49.3 us
    pallas_call x1, Pallas kernels: 56.5 us -> 47.7 us  [local_step(): pl.pallas_call(verify_kernel, out_shape=[vmem((4, 4, n_ids), F32), vmem((...]
    pallas_call x1, Pallas kernels: 4.23 us -> 1.68 us  [local_step(): pl.pallas_call(finish_kernel, out_shape=[jax.ShapeDtypeStruct((4, 4), F32...]
where the time goes in v3:
time: 50.1 us; the launch traced here: 50 us
  Pallas kernels  49.3 us (98%)
  between operations  0.64 us (1%)
    pallas_call x1, Pallas kernels, local_step(): pl.pallas_call(verify_kernel, out_shape=[vmem((4, 4, n_ids), F32), vmem((...  47.7 us
    pallas_call x1, Pallas kernels, local_step(): pl.pallas_call(finish_kernel, out_shape=[jax.ShapeDtypeStruct((4, 4), F32...  1.68 us

profile of v3, /device:TPU:0, one launch (start us, length us, event | category | flops | bytes accessed | tf_op | source)
XLA Modules:
  0.0 50.0 jit_solution(2017664472141663609)
XLA Ops:
  0.6 47.7 %verify.1 = (f32[4,4,37984]{2,1,0:T(4,128)S(1)}, f32[4,128]{1,0:T(4,128)S(1)}, f32[4,128]{1,0:T(4,128)S(1)}, f32[8,128]{1,0:T(8,128)S(1)}) custom-call(bf16[5,4,2048]{2,1,0:T(4,128)(2,1)} %bitcast.4, f32[1,2048]{1,0:T(1,128)} %bitcast.5, f32[4]{0:T(128)} %t_hbm.1, s32[4,4]{1,0:T(4,128)} %dt_hbm.1, bf16[37984,2048]{1,0:T(8,128)(2,1)} %bitcast.2.w_ref, ...), custom_call_target="tpu_custom_call" | custom-call | tf_op jit(solution)/shard_map/verify/pallas_call | solution.py:347
  48.3 1.7 %finish.1 = (f32[4,4]{1,0:T(4,128)}, f32[4,4]{1,0:T(4,128)}, f32[4,4,37984]{2,1,0:T(4,128)}, f32[1,4]{1,0:T(1,128)}) custom-call(f32[4,4,37984]{2,1,0:T(4,128)S(1)} %get-tuple-element.12.ex_ref, f32[4,128]{1,0:T(4,128)S(1)} %get-tuple-element.13.norm_ref, f32[4,128]{1,0:T(4,128)S(1)} %get-tuple-element.14.acc_ref, f32[8,128]{1,0:T(8,128)S(1)} %get-tuple-element.15.lse_ref), custom_call_target="tpu_custom_call" | custom-call | tf_op jit(solution)/shard_map/finish/pallas_call | solution.py:390

commit v4 on v3

--- a/solution.py
+++ b/solution.py
@@ -12,8 +12,8 @@
 TILE = 1024
 SUB = 256
 SLOTS = 4
-SHARED = 14
-FIRST = 5
+SHARED = 11
+FIRST = 8
 PASS = 1024
 
 

time: 50.1 us -> 54 us (1.078)
  Pallas kernels: 49.3 us -> 53.2 us
    pallas_call x1, Pallas kernels: 47.7 us -> 51.5 us  [local_step(): pl.pallas_call(verify_kernel, out_shape=[vmem((4, 4, n_ids), F32), vmem((...]
where the time goes in v4:
time: 54 us; the launch traced here: 53.9 us
  Pallas kernels  53.2 us (99%)
  between operations  0.64 us (1%)
    pallas_call x1, Pallas kernels, local_step(): pl.pallas_call(verify_kernel, out_shape=[vmem((4, 4, n_ids), F32), vmem((...  51.5 us
    pallas_call x1, Pallas kernels, local_step(): pl.pallas_call(finish_kernel, out_shape=[jax.ShapeDtypeStruct((4, 4), F32...  1.68 us

profile of v4, /device:TPU:0, one launch (start us, length us, event | category | flops | bytes accessed | tf_op | source)
XLA Modules:
  0.0 53.9 jit_solution(7306619227344954025)
XLA Ops:
  0.6 51.5 %verify.1 = (f32[4,4,37984]{2,1,0:T(4,128)S(1)}, f32[4,128]{1,0:T(4,128)S(1)}, f32[4,128]{1,0:T(4,128)S(1)}, f32[8,128]{1,0:T(8,128)S(1)}) custom-call(bf16[5,4,2048]{2,1,0:T(4,128)(2,1)} %bitcast.4, f32[1,2048]{1,0:T(1,128)} %bitcast.5, f32[4]{0:T(128)} %t_hbm.1, s32[4,4]{1,0:T(4,128)} %dt_hbm.1, bf16[37984,2048]{1,0:T(8,128)(2,1)} %bitcast.2.w_ref, ...), custom_call_target="tpu_custom_call" | custom-call | tf_op jit(solution)/shard_map/verify/pallas_call | solution.py:347
  52.2 1.7 %finish.1 = (f32[4,4]{1,0:T(4,128)}, f32[4,4]{1,0:T(4,128)}, f32[4,4,37984]{2,1,0:T(4,128)}, f32[1,4]{1,0:T(1,128)}) custom-call(f32[4,4,37984]{2,1,0:T(4,128)S(1)} %get-tuple-element.12.ex_ref, f32[4,128]{1,0:T(4,128)S(1)} %get-tuple-element.13.norm_ref, f32[4,128]{1,0:T(4,128)S(1)} %get-tuple-element.14.acc_ref, f32[8,128]{1,0:T(8,128)S(1)} %get-tuple-element.15.lse_ref), custom_call_target="tpu_custom_call" | custom-call | tf_op jit(solution)/shard_map/finish/pallas_call | solution.py:390

commit v5 on v3

--- a/solution.py
+++ b/solution.py
@@ -11,6 +11,7 @@
 
 TILE = 1024
 SUB = 256
+DEPTH = 256
 SLOTS = 4
 SHARED = 14
 FIRST = 5
@@ -20,14 +21,14 @@
 def verify_kernel(
     h_hbm, g_hbm, t_hbm, dt_hbm, w_ref, q_ref,
     ex_ref, norm_ref, acc_ref, lse_ref,
-    h_ref, g_ref, t_ref, dt_ref, wbuf, wtail, qv, s_scr, xf, xp, xrows, xb, tv, tp_recv, ct, dl, m_scr, l_scr, k_scr,
+    h_ref, g_ref, t_ref, dt_ref, wbuf, wtail, qv, s_scr, xf, xp, xrows, xb, xt, tv, tp_recv, ct, dl, m_scr, l_scr, k_scr,
     zsend, pstat_s, pstat_r, e1s, e1r, e2s, e2r, e3s, e3r,
     in_sem, w_sem, wt_sem, q_sem, x_sem, t_sem, zs_sem, zr_sem, ps_sem, e1_sem, e2_sem, e3_sem,
 ):
     dp, tp = lax.axis_index("dp"), lax.axis_index("tp")
     partner = (1 - dp, tp)
     peers = [(dp, lax.rem(tp + d, 4)) for d in (1, 2, 3)]
-    n_ids = w_ref.shape[0]
+    n_ids, width = w_ref.shape
     n_full = n_ids // TILE
     tail = n_ids - n_full * TILE
     tail_at = n_full * TILE
@@ -88,8 +89,14 @@
             dl[at + 8 * b : at + 8 * b + 8, :] = jnp.full((8, 128), -1.0, F32)
             for j in range(4):
                 dl[at + 8 * b + j : at + 8 * b + j + 1, :] = t_src[1 + j, b : b + 1, :] - lane.astype(F32)
-        xb[at : at + 32, :] = xrows[...].astype(jnp.bfloat16)
-
+        rows = xrows[...].astype(jnp.bfloat16)
+        xb[at : at + 32, :] = rows
+        for k in range(0, width, 128):
+            block = jnp.concatenate([xrows[:, k : k + 128], jnp.zeros((96, 128), F32)], axis=0).T
+            both = block if at == 0 else xt[k : k + 128, :].astype(F32) + pltpu.roll(block, at, 1)
+            xt[k : k + 128, :] = both.astype(jnp.bfloat16)
+
+    xb[32:64, :] = jnp.zeros((32, width), jnp.bfloat16)
     lay_rows(xf, tv, 0)
     m_scr[...] = jnp.full(m_scr.shape, LOWEST, F32)
     l_scr[...] = jnp.zeros_like(l_scr)
@@ -105,8 +112,26 @@
     x_copy.start()
     t_copy.start()
 
-    def product(rows, w):
-        return lax.dot_general(xb[0:rows, :], w, (((1,), (1,)), ((), ())), preferred_element_type=F32)
+    def by_rows(w, depth):
+        return lax.dot_general(xb[:, depth], w, (((1,), (1,)), ((), ())), preferred_element_type=F32)
+
+    def by_ids(w, depth):
+        return lax.dot_general(w, xt[depth, :], (((1,), (0,)), ((), ())), preferred_element_type=F32)
+
+    def tile_products(slot):
+        sums = [None] * 4
+        for k in range(0, width, DEPTH):
+            depth = slice(k, k + DEPTH)
+            for q in range(4):
+                w = wbuf[slot, q * SUB : (q + 1) * SUB, depth]
+                z = by_rows(w, depth) if q < 2 else by_ids(w, depth)
+                sums[q] = z if k == 0 else sums[q] + z
+        pieces = []
+        for z in sums[:2]:
+            pieces += [z[:, 0:128], z[:, 128:256]]
+        for z in sums[2:]:
+            pieces += [z[at : at + 128, :].T[0:64] for at in (0, 128)]
+        return pieces
 
     def fold(rows, parts):
         m_old = m_scr[0:rows, :]
@@ -120,8 +145,7 @@
         l_scr[0:rows, :] = total
 
     tail_copy.wait()
-    z = product(32, wtail[...])
-    s = z * ct[0:32, 0:tail]
+    s = by_rows(wtail[...], slice(0, width))[0:32] * ct[0:32, 0:tail]
     for b in range(4):
         s_scr[b, :, tail_at : tail_at + tail] = s[8 * b : 8 * b + 4, :]
     k_scr[0:32, 0:tail] = jnp.where(dl[0:32, 0:tail] == float(tail_at), s, 0.0)
@@ -151,19 +175,19 @@
 
         at = column(i)
         kept = k_scr[0:rows, :]
-        for c in range(TILE // SUB):
-            z = product(rows, wbuf[slot, c * SUB : (c + 1) * SUB, :])
-            parts = []
-            for lane in range(0, SUB, 128):
-                s = z[:, lane : lane + 128] * ct[0:rows, :]
-                parts.append(s)
-                off = c * SUB + lane
-                kept = jnp.where(dl[0:rows, :] == (at + off).astype(F32), s, kept)
-                for b in range(4):
-                    s_scr[b, :, pl.ds(at + off, 128)] = s[8 * b : 8 * b + 4, :]
-                    if rows == 64:
-                        zsend[k, b, :, off : off + 128] = s[32 + 8 * b : 32 + 8 * b + 4, :]
-            fold(rows, parts)
+        parts = []
+        for n, z in enumerate(tile_products(slot)):
+            s = z[0:rows] * ct[0:rows, :]
+            parts.append(s)
+            off = n * 128
+            kept = jnp.where(dl[0:rows, :] == (at + off).astype(F32), s, kept)
+            for b in range(4):
+                s_scr[b, :, pl.ds(at + off, 128)] = s[8 * b : 8 * b + 4, :]
+                if rows == 64:
+                    zsend[k, b, :, off : off + 128] = s[32 + 8 * b : 32 + 8 * b + 4, :]
+            if n % 2:
+                fold(rows, parts)
+                parts = []
         k_scr[0:rows, :] = kept
 
         @pl.when(i + SLOTS < steps)
@@ -362,6 +386,7 @@
                 vmem((5, 4, width), F32),
                 vmem((32, width), F32),
                 vmem((64, width), jnp.bfloat16),
+                vmem((width, 128), jnp.bfloat16),
                 vmem((5, 4, 128), F32),
                 vmem((5, 4, 128), F32),
                 vmem((64, 128), F32),

time: 50.1 us -> 47.9 us (0.956)
  Pallas kernels: 49.3 us -> 47.2 us
    pallas_call x1, Pallas kernels: 47.7 us -> 45.5 us  [local_step(): pl.pallas_call(verify_kernel, out_shape=[vmem((4, 4, n_ids), F32), vmem((...]
where the time goes in v5:
time: 47.9 us; the launch traced here: 47.8 us
  Pallas kernels  47.2 us (99%)
  between operations  0.64 us (1%)
    pallas_call x1, Pallas kernels, local_step(): pl.pallas_call(verify_kernel, out_shape=[vmem((4, 4, n_ids), F32), vmem((...  45.5 us
    pallas_call x1, Pallas kernels, local_step(): pl.pallas_call(finish_kernel, out_shape=[jax.ShapeDtypeStruct((4, 4), F32...  1.68 us

profile of v5, /device:TPU:0, one launch (start us, length us, event | category | flops | bytes accessed | tf_op | source)
XLA Modules:
  0.0 47.8 jit_solution(4593372727444521385)
XLA Ops:
  0.6 45.5 %verify.1 = (f32[4,4,37984]{2,1,0:T(4,128)S(1)}, f32[4,128]{1,0:T(4,128)S(1)}, f32[4,128]{1,0:T(4,128)S(1)}, f32[8,128]{1,0:T(8,128)S(1)}) custom-call(bf16[5,4,2048]{2,1,0:T(4,128)(2,1)} %bitcast.4, f32[1,2048]{1,0:T(1,128)} %bitcast.5, f32[4]{0:T(128)} %t_hbm.1, s32[4,4]{1,0:T(4,128)} %dt_hbm.1, bf16[37984,2048]{1,0:T(8,128)(2,1)} %bitcast.2.w_ref, ...), custom_call_target="tpu_custom_call" | custom-call | tf_op jit(solution)/shard_map/verify/pallas_call | solution.py:371
  46.1 1.7 %finish.1 = (f32[4,4]{1,0:T(4,128)}, f32[4,4]{1,0:T(4,128)}, f32[4,4,37984]{2,1,0:T(4,128)}, f32[1,4]{1,0:T(1,128)}) custom-call(f32[4,4,37984]{2,1,0:T(4,128)S(1)} %get-tuple-element.12.ex_ref, f32[4,128]{1,0:T(4,128)S(1)} %get-tuple-element.13.norm_ref, f32[4,128]{1,0:T(4,128)S(1)} %get-tuple-element.14.acc_ref, f32[8,128]{1,0:T(8,128)S(1)} %get-tuple-element.15.lse_ref), custom_call_target="tpu_custom_call" | custom-call | tf_op jit(solution)/shard_map/finish/pallas_call | solution.py:415

commit v6 on v5

--- a/solution.py
+++ b/solution.py
@@ -13,7 +13,7 @@
 SUB = 256
 DEPTH = 256
 SLOTS = 4
-SHARED = 14
+SHARED = 12
 FIRST = 5
 PASS = 1024
 

time: 47.9 us -> 45.4 us (0.948)
  Pallas kernels: 47.2 us -> 44.6 us
    pallas_call x1, Pallas kernels: 45.5 us -> 42.9 us  [local_step(): pl.pallas_call(verify_kernel, out_shape=[vmem((4, 4, n_ids), F32), vmem((...]
where the time goes in v6:
time: 45.4 us; the launch traced here: 45.3 us
  Pallas kernels  44.6 us (98%)
  between operations  0.64 us (1%)
    pallas_call x1, Pallas kernels, local_step(): pl.pallas_call(verify_kernel, out_shape=[vmem((4, 4, n_ids), F32), vmem((...  42.9 us
    pallas_call x1, Pallas kernels, local_step(): pl.pallas_call(finish_kernel, out_shape=[jax.ShapeDtypeStruct((4, 4), F32...  1.68 us

profile of v6, /device:TPU:0, one launch (start us, length us, event | category | flops | bytes accessed | tf_op | source)
XLA Modules:
  0.0 45.3 jit_solution(6650650273352005142)
XLA Ops:
  0.6 42.9 %verify.1 = (f32[4,4,37984]{2,1,0:T(4,128)S(1)}, f32[4,128]{1,0:T(4,128)S(1)}, f32[4,128]{1,0:T(4,128)S(1)}, f32[8,128]{1,0:T(8,128)S(1)}) custom-call(bf16[5,4,2048]{2,1,0:T(4,128)(2,1)} %bitcast.4, f32[1,2048]{1,0:T(1,128)} %bitcast.5, f32[4]{0:T(128)} %t_hbm.1, s32[4,4]{1,0:T(4,128)} %dt_hbm.1, bf16[37984,2048]{1,0:T(8,128)(2,1)} %bitcast.2.w_ref, ...), custom_call_target="tpu_custom_call" | custom-call | tf_op jit(solution)/shard_map/verify/pallas_call | solution.py:371
  43.6 1.7 %finish.1 = (f32[4,4]{1,0:T(4,128)}, f32[4,4]{1,0:T(4,128)}, f32[4,4,37984]{2,1,0:T(4,128)}, f32[1,4]{1,0:T(1,128)}) custom-call(f32[4,4,37984]{2,1,0:T(4,128)S(1)} %get-tuple-element.12.ex_ref, f32[4,128]{1,0:T(4,128)S(1)} %get-tuple-element.13.norm_ref, f32[4,128]{1,0:T(4,128)S(1)} %get-tuple-element.14.acc_ref, f32[8,128]{1,0:T(8,128)S(1)} %get-tuple-element.15.lse_ref), custom_call_target="tpu_custom_call" | custom-call | tf_op jit(solution)/shard_map/finish/pallas_call | solution.py:415

commit v7 on v5

--- a/solution.py
+++ b/solution.py
@@ -15,6 +15,7 @@
 SLOTS = 4
 SHARED = 14
 FIRST = 5
+RELAY = 3
 PASS = 1024
 
 
@@ -92,10 +93,9 @@
         rows = xrows[...].astype(jnp.bfloat16)
         xb[at : at + 32, :] = rows
         for k in range(0, width, 128):
-            block = jnp.concatenate([xrows[:, k : k + 128], jnp.zeros((96, 128), F32)], axis=0).T
-            both = block if at == 0 else xt[k : k + 128, :].astype(F32) + pltpu.roll(block, at, 1)
-            xt[k : k + 128, :] = both.astype(jnp.bfloat16)
-
+            xt[k : k + 128, at : at + 32] = xrows[:, k : k + 128].T.astype(jnp.bfloat16)
+
+    xt[:, 32:128] = jnp.zeros((width, 96), jnp.bfloat16)
     xb[32:64, :] = jnp.zeros((32, width), jnp.bfloat16)
     lay_rows(xf, tv, 0)
     m_scr[...] = jnp.full(m_scr.shape, LOWEST, F32)
@@ -103,13 +103,24 @@
     k_scr[...] = jnp.zeros_like(k_scr)
 
     pl.semaphore_wait(barrier, 4)
-    x_copy = pltpu.make_async_remote_copy(
-        src_ref=xf, dst_ref=xp, send_sem=x_sem.at[0], recv_sem=x_sem.at[1], device_id=partner, device_id_type=MESH
-    )
+    core = lax.rem(tp, 2)
+    sibling = (dp, tp + 1 - 2 * core)
+
+    def width_half(ref, c):
+        return ref.at[:, :, pl.ds(pl.multiple_of(c * (width // 2), width // 2), width // 2)]
+
+    def x_copy(src, c, to, k):
+        return pltpu.make_async_remote_copy(
+            src_ref=width_half(src, c), dst_ref=width_half(xp, c), send_sem=x_sem.at[0, k], recv_sem=x_sem.at[1, k],
+            device_id=to, device_id_type=MESH,
+        )
+
+    x_direct = x_copy(xf, core, partner, 0)
+    x_relay = x_copy(xp, core, sibling, 1)
     t_copy = pltpu.make_async_remote_copy(
         src_ref=tv, dst_ref=tp_recv, send_sem=t_sem.at[0], recv_sem=t_sem.at[1], device_id=partner, device_id_type=MESH
     )
-    x_copy.start()
+    x_direct.start()
     t_copy.start()
 
     def by_rows(w, depth):
@@ -166,13 +177,7 @@
         slot = i % SLOTS
         for c in tile_copies(i, slot):
             c.wait()
-        if rows == 64:
-            k = i - FIRST
-
-            @pl.when(k > 0)
-            def _():
-                z_copy(k - 1).start()
-
+        k = i - FIRST
         at = column(i)
         kept = k_scr[0:rows, :]
         parts = []
@@ -195,15 +200,21 @@
             for c in tile_copies(i + SLOTS, slot):
                 c.start()
 
-    lax.fori_loop(0, FIRST, lambda i, _: step(i, 32), None)
-    x_copy.wait()
+        if rows == 64:
+            z_copy(k).start()
+
+    lax.fori_loop(0, RELAY, lambda i, _: step(i, 32), None)
+    x_direct.wait()
+    x_relay.start()
+    lax.fori_loop(RELAY, FIRST, lambda i, _: step(i, 32), None)
+    x_copy(xp, 1 - core, sibling, 1).wait_recv()
+    x_relay.wait_send()
     t_copy.wait()
     lay_rows(xp, tp_recv, 32)
     lax.fori_loop(FIRST, FIRST + SHARED, lambda i, _: step(i, 64), None)
     pstat_s[0] = m_scr[32:64, :]
     pstat_s[1] = l_scr[32:64, :]
     pstat_s[2] = k_scr[32:64, :]
-    z_copy(SHARED - 1).start()
     stat_copy = pltpu.make_async_remote_copy(
         src_ref=pstat_s, dst_ref=pstat_r, send_sem=ps_sem.at[0], recv_sem=ps_sem.at[1],
         device_id=partner, device_id_type=MESH,
@@ -247,21 +258,37 @@
     q_copy.wait()
     own = [dl[8 * b : 8 * b + 4, :] for b in range(4)]
 
-    def pick(i, found):
-        at = pl.multiple_of(i * PASS, PASS)
+    row_m = [jnp.broadcast_to(row_max[8 * b : 8 * b + 4, :], (4, 128)) for b in range(4)]
+
+    def prepare(b, at, size, found):
+        s_scr[b, :, pl.ds(at, size)] = jnp.exp(s_scr[b, :, pl.ds(at, size)] - row_m[b][:, :size])
+        return jnp.where(own[b][:, :size] == jnp.asarray(at).astype(F32), qv[b, :, pl.ds(at, size)], found)
+
+    def prepare_tile(at, found):
         out = []
         for b in range(4):
             f = found[b]
-            for off in range(0, PASS, 128):
-                f = jnp.where(own[b] == (at + off).astype(F32), qv[b, :, pl.ds(at + off, 128)], f)
+            for off in range(0, TILE, 128):
+                f = prepare(b, at + off, 128, f)
             out.append(f)
         return tuple(out)
 
     zero = jnp.zeros((4, 128), F32)
-    found = lax.fori_loop(0, tail_at // PASS, pick, (zero,) * 4)
+    found = lax.fori_loop(0, steps, lambda i, f: prepare_tile(column(i), f), (zero,) * 4)
+
+    def take_z(k, found):
+        z_copy(k).wait_send()
+        at = pl.multiple_of((FIRST + (1 - dp) * SHARED + k) * TILE, TILE)
+        pltpu.make_async_remote_copy(
+            src_ref=zsend.at[k], dst_ref=s_scr.at[:, :, pl.ds(at, TILE)], send_sem=zs_sem.at[k], recv_sem=zr_sem.at[k],
+            device_id=partner, device_id_type=MESH,
+        ).wait_recv()
+        return prepare_tile(at, found)
+
+    found = lax.fori_loop(0, SHARED, take_z, found)
     token_q, token_s = [], []
     for b in range(4):
-        f = jnp.where(own[b][:, :tail] == float(tail_at), qv[b, :, tail_at : tail_at + tail], 0.0)
+        f = prepare(b, tail_at, tail, jnp.zeros((4, tail), F32))
         token_q.append(jnp.sum(found[b], axis=1, keepdims=True) + jnp.sum(f, axis=1, keepdims=True))
         kept = k_scr[8 * b : 8 * b + 4, :] + pstat_r[2, 8 * b : 8 * b + 4, :]
         token_s.append(jnp.sum(kept, axis=1, keepdims=True))
@@ -271,15 +298,6 @@
     for c in e3:
         c.start()
 
-    def await_z(k, _):
-        z_copy(k).wait_send()
-        pltpu.make_async_remote_copy(
-            src_ref=zsend.at[k], dst_ref=s_scr.at[:, :, pl.ds(pl.multiple_of((FIRST + (1 - dp) * SHARED + k) * TILE, TILE), TILE)],
-            send_sem=zs_sem.at[k], recv_sem=zr_sem.at[k], device_id=partner, device_id_type=MESH,
-        ).wait_recv()
-        return None
-
-    lax.fori_loop(0, SHARED, await_z, None)
     for c in e1:
         c.wait()
     lses = [e1s[...]] + [e1r[d] for d in range(3)]
@@ -287,10 +305,10 @@
     sums = jnp.exp(lses[0] - top) + jnp.exp(lses[1] - top) + jnp.exp(lses[2] - top) + jnp.exp(lses[3] - top)
     lse = top + jnp.log(sums)
     lse_ref[...] = lse
-    row_l = [jnp.broadcast_to(unpack(lse[0:4, :], b), (4, 128)) for b in range(4)]
+    scale = [jnp.exp(row_m[b] - jnp.broadcast_to(unpack(lse[0:4, :], b), (4, 128))) for b in range(4)]
 
     def excess(b, at, size):
-        e = jnp.maximum(jnp.exp(s_scr[b, :, pl.ds(at, size)] - row_l[b][:, :size]) - qv[b, :, pl.ds(at, size)], 0.0)
+        e = jnp.maximum(s_scr[b, :, pl.ds(at, size)] * scale[b][:, :size] - qv[b, :, pl.ds(at, size)], 0.0)
         ex_ref[b, :, pl.ds(at, size)] = e
         return e
 
@@ -403,7 +421,7 @@
                 vmem((3, 4, 128), F32),
                 vmem((2, 4, 128), F32),
                 vmem((3, 2, 4, 128), F32),
-                dma((4,)), dma((SLOTS, 2)), dma, dma, dma((2,)), dma((2,)), dma((SHARED,)), dma((SHARED,)), dma((2,)),
+                dma((4,)), dma((SLOTS, 2)), dma, dma, dma((2, 2)), dma((2,)), dma((SHARED,)), dma((SHARED,)), dma((2,)),
                 dma((2, 3)), dma((2, 3)), dma((2, 3)),
             ],
             compiler_params=pltpu.CompilerParams(collective_id=0, has_side_effects=True),

time: 47.9 us -> 56.3 us (1.18)
  Pallas kernels: 47.2 us -> 55.5 us
    pallas_call x1, Pallas kernels: 45.5 us -> 53.8 us  [local_step(): pl.pallas_call(verify_kernel, out_shape=[vmem((4, 4, n_ids), F32), vmem((...]
where the time goes in v7:
time: 56.3 us; the launch traced here: 56.2 us
  Pallas kernels  55.5 us (99%)
  between operations  0.64 us (1%)
    pallas_call x1, Pallas kernels, local_step(): pl.pallas_call(verify_kernel, out_shape=[vmem((4, 4, n_ids), F32), vmem((...  53.8 us
    pallas_call x1, Pallas kernels, local_step(): pl.pallas_call(finish_kernel, out_shape=[jax.ShapeDtypeStruct((4, 4), F32...  1.68 us

profile of v7, /device:TPU:0, one launch (start us, length us, event | category | flops | bytes accessed | tf_op | source)
XLA Modules:
  0.0 56.2 jit_solution(14996220813738430865)
XLA Ops:
  0.6 53.8 %verify.1 = (f32[4,4,37984]{2,1,0:T(4,128)S(1)}, f32[4,128]{1,0:T(4,128)S(1)}, f32[4,128]{1,0:T(4,128)S(1)}, f32[8,128]{1,0:T(8,128)S(1)}) custom-call(bf16[5,4,2048]{2,1,0:T(4,128)(2,1)} %bitcast.4, f32[1,2048]{1,0:T(1,128)} %bitcast.5, f32[4]{0:T(128)} %t_hbm.1, s32[4,4]{1,0:T(4,128)} %dt_hbm.1, bf16[37984,2048]{1,0:T(8,128)(2,1)} %bitcast.2.w_ref, ...), custom_call_target="tpu_custom_call" | custom-call | tf_op jit(solution)/shard_map/verify/pallas_call | solution.py:389
  54.5 1.7 %finish.1 = (f32[4,4]{1,0:T(4,128)}, f32[4,4]{1,0:T(4,128)}, f32[4,4,37984]{2,1,0:T(4,128)}, f32[1,4]{1,0:T(1,128)}) custom-call(f32[4,4,37984]{2,1,0:T(4,128)S(1)} %get-tuple-element.12.ex_ref, f32[4,128]{1,0:T(4,128)S(1)} %get-tuple-element.13.norm_ref, f32[4,128]{1,0:T(4,128)S(1)} %get-tuple-element.14.acc_ref, f32[8,128]{1,0:T(8,128)S(1)} %get-tuple-element.15.lse_ref), custom_call_target="tpu_custom_call" | custom-call | tf_op jit(solution)/shard_map/finish/pallas_call | solution.py:433

commit v8 on v7

--- a/solution.py
+++ b/solution.py
@@ -260,21 +260,19 @@
 
     row_m = [jnp.broadcast_to(row_max[8 * b : 8 * b + 4, :], (4, 128)) for b in range(4)]
 
-    def prepare(b, at, size, found):
-        s_scr[b, :, pl.ds(at, size)] = jnp.exp(s_scr[b, :, pl.ds(at, size)] - row_m[b][:, :size])
-        return jnp.where(own[b][:, :size] == jnp.asarray(at).astype(F32), qv[b, :, pl.ds(at, size)], found)
-
-    def prepare_tile(at, found):
-        out = []
-        for b in range(4):
-            f = found[b]
-            for off in range(0, TILE, 128):
-                f = prepare(b, at + off, 128, f)
-            out.append(f)
-        return tuple(out)
+    def prepare(at, size, found):
+        places = [(b, at + off, min(size, 128)) for b in range(4) for off in range(0, size, 128)]
+        values = [s_scr[b, :, pl.ds(a, n)] for b, a, n in places]
+        values = [jnp.exp(v - row_m[b][:, :n]) for v, (b, _, n) in zip(values, places)]
+        for v, (b, a, n) in zip(values, places):
+            s_scr[b, :, pl.ds(a, n)] = v
+        found = list(found)
+        for b, a, n in places:
+            found[b] = jnp.where(own[b][:, :n] == jnp.asarray(a).astype(F32), qv[b, :, pl.ds(a, n)], found[b])
+        return tuple(found)
 
     zero = jnp.zeros((4, 128), F32)
-    found = lax.fori_loop(0, steps, lambda i, f: prepare_tile(column(i), f), (zero,) * 4)
+    found = lax.fori_loop(0, steps, lambda i, f: prepare(column(i), TILE, f), (zero,) * 4)
 
     def take_z(k, found):
         z_copy(k).wait_send()
@@ -283,12 +281,13 @@
             src_ref=zsend.at[k], dst_ref=s_scr.at[:, :, pl.ds(at, TILE)], send_sem=zs_sem.at[k], recv_sem=zr_sem.at[k],
             device_id=partner, device_id_type=MESH,
         ).wait_recv()
-        return prepare_tile(at, found)
+        return prepare(at, TILE, found)
 
     found = lax.fori_loop(0, SHARED, take_z, found)
     token_q, token_s = [], []
+    found_tail = prepare(tail_at, tail, (jnp.zeros((4, tail), F32),) * 4)
     for b in range(4):
-        f = prepare(b, tail_at, tail, jnp.zeros((4, tail), F32))
+        f = found_tail[b]
         token_q.append(jnp.sum(found[b], axis=1, keepdims=True) + jnp.sum(f, axis=1, keepdims=True))
         kept = k_scr[8 * b : 8 * b + 4, :] + pstat_r[2, 8 * b : 8 * b + 4, :]
         token_s.append(jnp.sum(kept, axis=1, keepdims=True))

time: 56.3 us -> 47.5 us (0.84)
  Pallas kernels: 55.5 us -> 46.8 us
    pallas_call x1, Pallas kernels: 53.8 us -> 45.1 us  [local_step(): pl.pallas_call(verify_kernel, out_shape=[vmem((4, 4, n_ids), F32), vmem((...]
where the time goes in v8:
time: 47.5 us; the launch traced here: 47.4 us
  Pallas kernels  46.8 us (99%)
  between operations  0.64 us (1%)
    pallas_call x1, Pallas kernels, local_step(): pl.pallas_call(verify_kernel, out_shape=[vmem((4, 4, n_ids), F32), vmem((...  45.1 us
    pallas_call x1, Pallas kernels, local_step(): pl.pallas_call(finish_kernel, out_shape=[jax.ShapeDtypeStruct((4, 4), F32...  1.68 us

profile of v8, /device:TPU:0, one launch (start us, length us, event | category | flops | bytes accessed | tf_op | source)
XLA Modules:
  0.0 47.4 jit_solution(7239879119128475283)
XLA Ops:
  0.6 45.1 %verify.1 = (f32[4,4,37984]{2,1,0:T(4,128)S(1)}, f32[4,128]{1,0:T(4,128)S(1)}, f32[4,128]{1,0:T(4,128)S(1)}, f32[8,128]{1,0:T(8,128)S(1)}) custom-call(bf16[5,4,2048]{2,1,0:T(4,128)(2,1)} %bitcast.4, f32[1,2048]{1,0:T(1,128)} %bitcast.5, f32[4]{0:T(128)} %t_hbm.1, s32[4,4]{1,0:T(4,128)} %dt_hbm.1, bf16[37984,2048]{1,0:T(8,128)(2,1)} %bitcast.2.w_ref, ...), custom_call_target="tpu_custom_call" | custom-call | tf_op jit(solution)/shard_map/verify/pallas_call | solution.py:388
  45.7 1.7 %finish.1 = (f32[4,4]{1,0:T(4,128)}, f32[4,4]{1,0:T(4,128)}, f32[4,4,37984]{2,1,0:T(4,128)}, f32[1,4]{1,0:T(1,128)}) custom-call(f32[4,4,37984]{2,1,0:T(4,128)S(1)} %get-tuple-element.12.ex_ref, f32[4,128]{1,0:T(4,128)S(1)} %get-tuple-element.13.norm_ref, f32[4,128]{1,0:T(4,128)S(1)} %get-tuple-element.14.acc_ref, f32[8,128]{1,0:T(8,128)S(1)} %get-tuple-element.15.lse_ref), custom_call_target="tpu_custom_call" | custom-call | tf_op jit(solution)/shard_map/finish/pallas_call | solution.py:432

commit v9 on v8

--- a/solution.py
+++ b/solution.py
@@ -15,6 +15,7 @@
 SLOTS = 4
 SHARED = 14
 FIRST = 5
+HELD = 2
 RELAY = 3
 PASS = 1024
 
@@ -201,7 +202,34 @@
                 c.start()
 
         if rows == 64:
-            z_copy(k).start()
+
+            @pl.when(k < SHARED - HELD)
+            def _():
+                z_copy(k).start()
+
+    group = lax.broadcasted_iota(jnp.int32, (8, 128), 1) // 32
+
+    def pack(cols):
+        size = cols[0].shape[0]
+        packed = jnp.broadcast_to(cols[0], (size, 128))
+        for b in range(1, 4):
+            packed = jnp.where(group[:size] == b, cols[b], packed)
+        return packed
+
+    def unpack(packed, b):
+        size = packed.shape[0]
+        lane = lax.broadcasted_iota(jnp.int32, (size, 128), 1)
+        return jnp.sum(jnp.where(lane == 32 * b, packed, 0.0), axis=1, keepdims=True)
+
+    def packed_lse(at):
+        m = m_scr[at : at + 32, :]
+        top = jnp.max(m, axis=1, keepdims=True)
+        lse = top + jnp.log(jnp.sum(l_scr[at : at + 32, :] * jnp.exp(m - top), axis=1, keepdims=True))
+        return pack([lse[8 * b : 8 * b + 8, :] for b in range(4)])
+
+    def packed_token(at):
+        kept = jnp.sum(k_scr[at : at + 32, :], axis=1, keepdims=True)
+        return pack([kept[8 * b : 8 * b + 8, :] for b in range(4)])
 
     lax.fori_loop(0, RELAY, lambda i, _: step(i, 32), None)
     x_direct.wait()
@@ -212,29 +240,16 @@
     t_copy.wait()
     lay_rows(xp, tp_recv, 32)
     lax.fori_loop(FIRST, FIRST + SHARED, lambda i, _: step(i, 64), None)
-    pstat_s[0] = m_scr[32:64, :]
-    pstat_s[1] = l_scr[32:64, :]
-    pstat_s[2] = k_scr[32:64, :]
+    pstat_s[0] = packed_lse(32)
+    pstat_s[1] = packed_token(32)
     stat_copy = pltpu.make_async_remote_copy(
         src_ref=pstat_s, dst_ref=pstat_r, send_sem=ps_sem.at[0], recv_sem=ps_sem.at[1],
         device_id=partner, device_id_type=MESH,
     )
     stat_copy.start()
+    for k in range(SHARED - HELD, SHARED):
+        z_copy(k).start()
     lax.fori_loop(FIRST + SHARED, steps, lambda i, _: step(i, 32), None)
-
-    group = lax.broadcasted_iota(jnp.int32, (8, 128), 1) // 32
-
-    def pack(cols):
-        size = cols[0].shape[0]
-        packed = jnp.broadcast_to(cols[0], (size, 128))
-        for b in range(1, 4):
-            packed = jnp.where(group[:size] == b, cols[b], packed)
-        return packed
-
-    def unpack(packed, b):
-        size = packed.shape[0]
-        lane = lax.broadcasted_iota(jnp.int32, (size, 128), 1)
-        return jnp.sum(jnp.where(lane == 32 * b, packed, 0.0), axis=1, keepdims=True)
 
     def exchange(src, dst, sem):
         return [
@@ -245,12 +260,12 @@
             for d in range(3)
         ]
 
+    mine = packed_lse(0)
     stat_copy.wait()
-    m = jnp.maximum(m_scr[0:32, :], pstat_r[0])
-    total = l_scr[0:32, :] * jnp.exp(m_scr[0:32, :] - m) + pstat_r[1] * jnp.exp(pstat_r[0] - m)
-    row_max = jnp.max(m, axis=1, keepdims=True)
-    row_lse = row_max + jnp.log(jnp.sum(total * jnp.exp(m - row_max), axis=1, keepdims=True))
-    e1s[...] = pack([row_lse[8 * b : 8 * b + 8, :] for b in range(4)])
+    theirs = pstat_r[0]
+    top = jnp.maximum(mine, theirs)
+    near = top + jnp.log(jnp.exp(mine - top) + jnp.exp(theirs - top))
+    e1s[...] = near
     e1 = exchange(e1s, e1r, e1_sem)
     for c in e1:
         c.start()
@@ -258,7 +273,7 @@
     q_copy.wait()
     own = [dl[8 * b : 8 * b + 4, :] for b in range(4)]
 
-    row_m = [jnp.broadcast_to(row_max[8 * b : 8 * b + 4, :], (4, 128)) for b in range(4)]
+    row_m = [jnp.broadcast_to(unpack(near[0:4, :], b), (4, 128)) for b in range(4)]
 
     def prepare(at, size, found):
         places = [(b, at + off, min(size, 128)) for b in range(4) for off in range(0, size, 128)]
@@ -284,14 +299,12 @@
         return prepare(at, TILE, found)
 
     found = lax.fori_loop(0, SHARED, take_z, found)
-    token_q, token_s = [], []
+    token_q = []
     found_tail = prepare(tail_at, tail, (jnp.zeros((4, tail), F32),) * 4)
     for b in range(4):
         f = found_tail[b]
         token_q.append(jnp.sum(found[b], axis=1, keepdims=True) + jnp.sum(f, axis=1, keepdims=True))
-        kept = k_scr[8 * b : 8 * b + 4, :] + pstat_r[2, 8 * b : 8 * b + 4, :]
-        token_s.append(jnp.sum(kept, axis=1, keepdims=True))
-    e3s[0] = pack(token_s)
+    e3s[0] = (packed_token(0) + pstat_r[1])[0:4, :]
     e3s[1] = pack(token_q)
     e3 = exchange(e3s, e3r, e3_sem)
     for c in e3:
@@ -299,7 +312,7 @@
 
     for c in e1:
         c.wait()
-    lses = [e1s[...]] + [e1r[d] for d in range(3)]
+    lses = [near] + [e1r[d] for d in range(3)]
     top = jnp.maximum(jnp.maximum(lses[0], lses[1]), jnp.maximum(lses[2], lses[3]))
     sums = jnp.exp(lses[0] - top) + jnp.exp(lses[1] - top) + jnp.exp(lses[2] - top) + jnp.exp(lses[3] - top)
     lse = top + jnp.log(sums)
@@ -412,8 +425,8 @@
                 vmem((64, 128), F32),
                 vmem((64, 128), F32),
                 vmem((SHARED, 4, 4, TILE), F32),
-                vmem((3, 32, 128), F32),
-                vmem((3, 32, 128), F32),
+                vmem((2, 8, 128), F32),
+                vmem((2, 8, 128), F32),
                 vmem((8, 128), F32),
                 vmem((3, 8, 128), F32),
                 vmem((4, 128), F32),

time: 47.5 us -> 44.5 us (0.937)
  Pallas kernels: 46.8 us -> 43.7 us
    pallas_call x1, Pallas kernels: 45.1 us -> 42 us  [local_step(): pl.pallas_call(verify_kernel, out_shape=[vmem((4, 4, n_ids), F32), vmem((...]
where the time goes in v9:
time: 44.5 us; the launch traced here: 44.4 us
  Pallas kernels  43.7 us (98%)
  between operations  0.64 us (1%)
    pallas_call x1, Pallas kernels, local_step(): pl.pallas_call(verify_kernel, out_shape=[vmem((4, 4, n_ids), F32), vmem((...  42 us
    pallas_call x1, Pallas kernels, local_step(): pl.pallas_call(finish_kernel, out_shape=[jax.ShapeDtypeStruct((4, 4), F32...  1.68 us

profile of v9, /device:TPU:0, one launch (start us, length us, event | category | flops | bytes accessed | tf_op | source)
XLA Modules:
  0.0 44.4 jit_solution(6176532359280767227)
XLA Ops:
  0.6 42.0 %verify.1 = (f32[4,4,37984]{2,1,0:T(4,128)S(1)}, f32[4,128]{1,0:T(4,128)S(1)}, f32[4,128]{1,0:T(4,128)S(1)}, f32[8,128]{1,0:T(8,128)S(1)}) custom-call(bf16[5,4,2048]{2,1,0:T(4,128)(2,1)} %bitcast.4, f32[1,2048]{1,0:T(1,128)} %bitcast.5, f32[4]{0:T(128)} %t_hbm.1, s32[4,4]{1,0:T(4,128)} %dt_hbm.1, bf16[37984,2048]{1,0:T(8,128)(2,1)} %bitcast.2.w_ref, ...), custom_call_target="tpu_custom_call" | custom-call | tf_op jit(solution)/shard_map/verify/pallas_call | solution.py:401
  42.7 1.7 %finish.1 = (f32[4,4]{1,0:T(4,128)}, f32[4,4]{1,0:T(4,128)}, f32[4,4,37984]{2,1,0:T(4,128)}, f32[1,4]{1,0:T(1,128)}) custom-call(f32[4,4,37984]{2,1,0:T(4,128)S(1)} %get-tuple-element.12.ex_ref, f32[4,128]{1,0:T(4,128)S(1)} %get-tuple-element.13.norm_ref, f32[4,128]{1,0:T(4,128)S(1)} %get-tuple-element.14.acc_ref, f32[8,128]{1,0:T(8,128)S(1)} %get-tuple-element.15.lse_ref), custom_call_target="tpu_custom_call" | custom-call | tf_op jit(solution)/shard_map/finish/pallas_call | solution.py:445

commit v10 on v9

--- a/solution.py
+++ b/solution.py
@@ -13,10 +13,10 @@
 SUB = 256
 DEPTH = 256
 SLOTS = 4
-SHARED = 14
-FIRST = 5
+SHARED = 13
+FIRST = 4
 HELD = 2
-RELAY = 3
+RELAY = 2
 PASS = 1024
 
 

time: 44.5 us -> 45.1 us (1.013)
  Pallas kernels: 43.7 us -> 44.4 us
    pallas_call x1, Pallas kernels: 42 us -> 42.7 us  [local_step(): pl.pallas_call(verify_kernel, out_shape=[vmem((4, 4, n_ids), F32), vmem((...]
where the time goes in v10:
time: 45.1 us; the launch traced here: 45 us
  Pallas kernels  44.4 us (98%)
  between operations  0.64 us (1%)
    pallas_call x1, Pallas kernels, local_step(): pl.pallas_call(verify_kernel, out_shape=[vmem((4, 4, n_ids), F32), vmem((...  42.7 us
    pallas_call x1, Pallas kernels, local_step(): pl.pallas_call(finish_kernel, out_shape=[jax.ShapeDtypeStruct((4, 4), F32...  1.68 us

profile of v10, /device:TPU:0, one launch (start us, length us, event | category | flops | bytes accessed | tf_op | source)
XLA Modules:
  0.0 45.0 jit_solution(4122934348604508340)
XLA Ops:
  0.6 42.7 %verify.1 = (f32[4,4,37984]{2,1,0:T(4,128)S(1)}, f32[4,128]{1,0:T(4,128)S(1)}, f32[4,128]{1,0:T(4,128)S(1)}, f32[8,128]{1,0:T(8,128)S(1)}) custom-call(bf16[5,4,2048]{2,1,0:T(4,128)(2,1)} %bitcast.4, f32[1,2048]{1,0:T(1,128)} %bitcast.5, f32[4]{0:T(128)} %t_hbm.1, s32[4,4]{1,0:T(4,128)} %dt_hbm.1, bf16[37984,2048]{1,0:T(8,128)(2,1)} %bitcast.2.w_ref, ...), custom_call_target="tpu_custom_call" | custom-call | tf_op jit(solution)/shard_map/verify/pallas_call | solution.py:401
  43.3 1.7 %finish.1 = (f32[4,4]{1,0:T(4,128)}, f32[4,4]{1,0:T(4,128)}, f32[4,4,37984]{2,1,0:T(4,128)}, f32[1,4]{1,0:T(1,128)}) custom-call(f32[4,4,37984]{2,1,0:T(4,128)S(1)} %get-tuple-element.12.ex_ref, f32[4,128]{1,0:T(4,128)S(1)} %get-tuple-element.13.norm_ref, f32[4,128]{1,0:T(4,128)S(1)} %get-tuple-element.14.acc_ref, f32[8,128]{1,0:T(8,128)S(1)} %get-tuple-element.15.lse_ref), custom_call_target="tpu_custom_call" | custom-call | tf_op jit(solution)/shard_map/finish/pallas_call | solution.py:445

commit v11 on v10

--- a/solution.py
+++ b/solution.py
@@ -13,11 +13,12 @@
 SUB = 256
 DEPTH = 256
 SLOTS = 4
-SHARED = 13
+SHARED = 14
 FIRST = 4
 HELD = 2
 RELAY = 2
-PASS = 1024
+PARTS = 4
+PASS = 4736
 
 
 def verify_kernel(
@@ -42,15 +43,15 @@
         past_shared = (i + steps - FIRST - SHARED) // steps
         return pl.multiple_of((i + in_shared * dp * SHARED + past_shared * (SHARED - dp * SHARED)) * TILE, TILE)
 
-    half = TILE // 2
+    part = TILE // PARTS
 
     def tile_copies(i, slot):
         at = column(i)
         return [
             pltpu.make_async_copy(
-                w_ref.at[pl.ds(at + k * half, half), :], wbuf.at[slot, pl.ds(k * half, half), :], w_sem.at[slot, k]
+                w_ref.at[pl.ds(at + k * part, part), :], wbuf.at[slot, pl.ds(k * part, part), :], w_sem.at[slot, k]
             )
-            for k in (0, 1)
+            for k in range(PARTS)
         ]
 
     tail_copy = pltpu.make_async_copy(w_ref.at[pl.ds(tail_at, tail), :], wtail, wt_sem)
@@ -65,7 +66,6 @@
     for i in range(SLOTS):
         for c in tile_copies(i, i):
             c.start()
-    q_copy.start()
 
     barrier = pltpu.get_barrier_semaphore()
     for other in [partner] + peers:
@@ -130,19 +130,21 @@
     def by_ids(w, depth):
         return lax.dot_general(w, xt[depth, :], (((1,), (0,)), ((), ())), preferred_element_type=F32)
 
-    def tile_products(slot):
-        sums = [None] * 4
+    def products(slot, lo, size):
+        block = min(SUB, size // 2)
+        starts = range(lo, lo + size, block)
+        fixed = len(starts) // 2
+        sums = [None] * len(starts)
         for k in range(0, width, DEPTH):
             depth = slice(k, k + DEPTH)
-            for q in range(4):
-                w = wbuf[slot, q * SUB : (q + 1) * SUB, depth]
-                z = by_rows(w, depth) if q < 2 else by_ids(w, depth)
-                sums[q] = z if k == 0 else sums[q] + z
+            for n, start in enumerate(starts):
+                w = wbuf[slot, start : start + block, depth]
+                z = by_rows(w, depth) if n < fixed else by_ids(w, depth)
+                sums[n] = z if k == 0 else sums[n] + z
         pieces = []
-        for z in sums[:2]:
-            pieces += [z[:, 0:128], z[:, 128:256]]
-        for z in sums[2:]:
-            pieces += [z[at : at + 128, :].T[0:64] for at in (0, 128)]
+        for n, z in enumerate(sums):
+            for at in range(0, block, 128):
+                pieces.append(z[:, at : at + 128] if n < fixed else z[at : at + 128, :].T[0:64])
         return pieces
 
     def fold(rows, parts):
@@ -174,18 +176,13 @@
             device_id=partner, device_id_type=MESH,
         )
 
-    def step(i, rows):
-        slot = i % SLOTS
-        for c in tile_copies(i, slot):
-            c.wait()
-        k = i - FIRST
-        at = column(i)
+    def consume(slot, at, lo, size, rows, k):
         kept = k_scr[0:rows, :]
         parts = []
-        for n, z in enumerate(tile_products(slot)):
+        for n, z in enumerate(products(slot, lo, size)):
             s = z[0:rows] * ct[0:rows, :]
             parts.append(s)
-            off = n * 128
+            off = lo + n * 128
             kept = jnp.where(dl[0:rows, :] == (at + off).astype(F32), s, kept)
             for b in range(4):
                 s_scr[b, :, pl.ds(at + off, 128)] = s[8 * b : 8 * b + 4, :]
@@ -196,6 +193,13 @@
                 parts = []
         k_scr[0:rows, :] = kept
 
+    def step(i, rows):
+        slot = i % SLOTS
+        for c in tile_copies(i, slot):
+            c.wait()
+        k = i - FIRST
+        consume(slot, column(i), 0, TILE, rows, k)
+
         @pl.when(i + SLOTS < steps)
         def _():
             for c in tile_copies(i + SLOTS, slot):
@@ -240,6 +244,7 @@
     t_copy.wait()
     lay_rows(xp, tp_recv, 32)
     lax.fori_loop(FIRST, FIRST + SHARED, lambda i, _: step(i, 64), None)
+    q_copy.start()
     pstat_s[0] = packed_lse(32)
     pstat_s[1] = packed_token(32)
     stat_copy = pltpu.make_async_remote_copy(
@@ -249,7 +254,13 @@
     stat_copy.start()
     for k in range(SHARED - HELD, SHARED):
         z_copy(k).start()
-    lax.fori_loop(FIRST + SHARED, steps, lambda i, _: step(i, 32), None)
+    lax.fori_loop(FIRST + SHARED, steps - 1, lambda i, _: step(i, 32), None)
+    end, slot = steps - 1, (steps - 1) % SLOTS
+    copies = tile_copies(end, slot)
+    for lo, size in ((0, 2 * part), (2 * part, part), (3 * part, part)):
+        for c in copies[lo // part : (lo + size) // part]:
+            c.wait()
+        consume(slot, column(end), lo, size, 32, 0)
 
     def exchange(src, dst, sem):
         return [
@@ -270,37 +281,34 @@
     for c in e1:
         c.start()
 
-    q_copy.wait()
     own = [dl[8 * b : 8 * b + 4, :] for b in range(4)]
 
     row_m = [jnp.broadcast_to(unpack(near[0:4, :], b), (4, 128)) for b in range(4)]
 
-    def prepare(at, size, found):
+    def prepare(at, size):
         places = [(b, at + off, min(size, 128)) for b in range(4) for off in range(0, size, 128)]
         values = [s_scr[b, :, pl.ds(a, n)] for b, a, n in places]
         values = [jnp.exp(v - row_m[b][:, :n]) for v, (b, _, n) in zip(values, places)]
         for v, (b, a, n) in zip(values, places):
             s_scr[b, :, pl.ds(a, n)] = v
-        found = list(found)
-        for b, a, n in places:
-            found[b] = jnp.where(own[b][:, :n] == jnp.asarray(a).astype(F32), qv[b, :, pl.ds(a, n)], found[b])
-        return tuple(found)
+
+    def pick(at, size, found):
+        out = []
+        for b in range(4):
+            f = found[b]
+            for off in range(0, size, 128):
+                n = min(size, 128)
+                f = jnp.where(own[b][:, :n] == jnp.asarray(at + off).astype(F32), qv[b, :, pl.ds(at + off, n)], f)
+            out.append(f)
+        return tuple(out)
 
     zero = jnp.zeros((4, 128), F32)
-    found = lax.fori_loop(0, steps, lambda i, f: prepare(column(i), TILE, f), (zero,) * 4)
-
-    def take_z(k, found):
-        z_copy(k).wait_send()
-        at = pl.multiple_of((FIRST + (1 - dp) * SHARED + k) * TILE, TILE)
-        pltpu.make_async_remote_copy(
-            src_ref=zsend.at[k], dst_ref=s_scr.at[:, :, pl.ds(at, TILE)], send_sem=zs_sem.at[k], recv_sem=zr_sem.at[k],
-            device_id=partner, device_id_type=MESH,
-        ).wait_recv()
-        return prepare(at, TILE, found)
-
-    found = lax.fori_loop(0, SHARED, take_z, found)
+    lax.fori_loop(0, steps, lambda i, _: prepare(column(i), TILE), None)
+    prepare(tail_at, tail)
+    q_copy.wait()
+    found = lax.fori_loop(0, tail_at // PASS, lambda i, f: pick(pl.multiple_of(i * PASS, 128), PASS, f), (zero,) * 4)
+    found_tail = pick(tail_at, tail, (jnp.zeros((4, tail), F32),) * 4)
     token_q = []
-    found_tail = prepare(tail_at, tail, (jnp.zeros((4, tail), F32),) * 4)
     for b in range(4):
         f = found_tail[b]
         token_q.append(jnp.sum(found[b], axis=1, keepdims=True) + jnp.sum(f, axis=1, keepdims=True))
@@ -310,6 +318,17 @@
     for c in e3:
         c.start()
 
+    def take_z(k, _):
+        z_copy(k).wait_send()
+        at = pl.multiple_of((FIRST + (1 - dp) * SHARED + k) * TILE, TILE)
+        pltpu.make_async_remote_copy(
+            src_ref=zsend.at[k], dst_ref=s_scr.at[:, :, pl.ds(at, TILE)], send_sem=zs_sem.at[k], recv_sem=zr_sem.at[k],
+            device_id=partner, device_id_type=MESH,
+        ).wait_recv()
+        prepare(at, TILE)
+
+    lax.fori_loop(0, SHARED, take_z, None)
+
     for c in e1:
         c.wait()
     lses = [near] + [e1r[d] for d in range(3)]
@@ -325,7 +344,7 @@
         return e
 
     def last_pass(i, sums):
-        at = pl.multiple_of(i * PASS, PASS)
+        at = pl.multiple_of(i * PASS, 128)
         out = []
         for b in range(4):
             acc = sums[b]
@@ -433,7 +452,7 @@
                 vmem((3, 4, 128), F32),
                 vmem((2, 4, 128), F32),
                 vmem((3, 2, 4, 128), F32),
-                dma((4,)), dma((SLOTS, 2)), dma, dma, dma((2, 2)), dma((2,)), dma((SHARED,)), dma((SHARED,)), dma((2,)),
+                dma((4,)), dma((SLOTS, PARTS)), dma, dma, dma((2, 2)), dma((2,)), dma((SHARED,)), dma((SHARED,)), dma((2,)),
                 dma((2, 3)), dma((2, 3)), dma((2, 3)),
             ],
             compiler_params=pltpu.CompilerParams(collective_id=0, has_side_effects=True),

time: 45.1 us -> 46 us (1.020)
  Pallas kernels: 44.4 us -> 45.3 us
    pallas_call x1, Pallas kernels: 42.7 us -> 43.6 us  [local_step(): pl.pallas_call(verify_kernel, out_shape=[vmem((4, 4, n_ids), F32), vmem((...]
where the time goes in v11:
time: 46 us; the launch traced here: 45.9 us
  Pallas kernels  45.3 us (98%)
  between operations  0.64 us (1%)
    pallas_call x1, Pallas kernels, local_step(): pl.pallas_call(verify_kernel, out_shape=[vmem((4, 4, n_ids), F32), vmem((...  43.6 us
    pallas_call x1, Pallas kernels, local_step(): pl.pallas_call(finish_kernel, out_shape=[jax.ShapeDtypeStruct((4, 4), F32...  1.68 us

profile of v11, /device:TPU:0, one launch (start us, length us, event | category | flops | bytes accessed | tf_op | source)
XLA Modules:
  0.0 45.9 jit_solution(10553489482622032733)
XLA Ops:
  0.6 43.6 %verify.1 = (f32[4,4,37984]{2,1,0:T(4,128)S(1)}, f32[4,128]{1,0:T(4,128)S(1)}, f32[4,128]{1,0:T(4,128)S(1)}, f32[8,128]{1,0:T(8,128)S(1)}) custom-call(bf16[5,4,2048]{2,1,0:T(4,128)(2,1)} %bitcast.4, f32[1,2048]{1,0:T(1,128)} %bitcast.5, f32[4]{0:T(128)} %t_hbm.1, s32[4,4]{1,0:T(4,128)} %dt_hbm.1, bf16[37984,2048]{1,0:T(8,128)(2,1)} %bitcast.2.w_ref, ...), custom_call_target="tpu_custom_call" | custom-call | tf_op jit(solution)/shard_map/verify/pallas_call | solution.py:420
  44.2 1.7 %finish.1 = (f32[4,4]{1,0:T(4,128)}, f32[4,4]{1,0:T(4,128)}, f32[4,4,37984]{2,1,0:T(4,128)}, f32[1,4]{1,0:T(1,128)}) custom-call(f32[4,4,37984]{2,1,0:T(4,128)S(1)} %get-tuple-element.12.ex_ref, f32[4,128]{1,0:T(4,128)S(1)} %get-tuple-element.13.norm_ref, f32[4,128]{1,0:T(4,128)S(1)} %get-tuple-element.14.acc_ref, f32[8,128]{1,0:T(8,128)S(1)} %get-tuple-element.15.lse_ref), custom_call_target="tpu_custom_call" | custom-call | tf_op jit(solution)/shard_map/finish/pallas_call | solution.py:464
